TPU v7x, 256 devices: a whole 4x4x8 slice. The times are simulated.
256 devices in a mesh: row: 8 (over z_hi, core), sa: 32 (over z_lo, x, y).
Axes of the slice: x: 4, y: 4, z: 8 (z_hi: 4, z_lo: 2; z = z_hi * 2 + z_lo), core: 2. Of those that a mesh axis runs over, the one named last changes fastest.
Arguments:
- rep_w1: float32 [16, 8, 128, 4096], P('row', None, None, 'sa'), may hold values from -6 to 6
- rep_w3: float32 [16, 8, 128, 4096], P('row', None, None, 'sa'), may hold values from -6 to 6
- rep_w2: float32 [16, 8, 128, 4096], P('row', None, None, 'sa'), may hold values from -6 to 6
- rep_gate: float32 [16, 8, 4096], P('row', None, 'sa'), may hold values from -6 to 6
Outputs:
- serve_w1: bfloat16 [8, 128, 4096], P('row', 'sa')
- serve_w3: bfloat16 [8, 128, 4096], P('row', 'sa')
- serve_w2: bfloat16 [8, 128, 4096], P('row', 'sa')
- serve_gate: bfloat16 [8, 4096], replicated
- soup_norms: float32 [8, 4], P('row')
- replica_norms: float32 [16, 8, 4], P('row')
All inputs are finite; a program needn't handle non-finite values.
Results may differ from a plain program's by a relative error of at most 0.001.
Values may be sent and summed in bfloat16 or wider, within the bound.
No kernel may reach another device: no remote copies, remote signals or barrier semaphores. Data moves between devices by JAX's collectives and lax.ppermute only.
A program may use at most 64 MiB of HBM per device.

v0:
```python
import functools

import jax
import jax.numpy as jnp
from jax import lax
from jax.experimental import pallas as pl
from jax.experimental.pallas import tpu as pltpu
from jax.sharding import Mesh
from jax.sharding import PartitionSpec as P


ROW = ("zh", "c")
SA = ("zl", "x", "y")
SCALE = 2048.0
STEPS = (2, 1, 3)
ROOM = 6 << 20
F32 = jnp.float32


def call(kernel, out_shape, flops, scratch=(), in_hbm=0):
    def run(*args):
        specs = [pl.BlockSpec(memory_space=pltpu.HBM)] * in_hbm
        specs += [pl.BlockSpec(memory_space=pltpu.VMEM)] * (len(args) - in_hbm)
        return pl.pallas_call(
            kernel,
            out_shape=out_shape,
            in_specs=specs,
            out_specs=jax.tree.map(lambda _: pl.BlockSpec(memory_space=pltpu.VMEM), out_shape),
            scratch_shapes=scratch,
            compiler_params=pltpu.CompilerParams(vmem_limit_bytes=ROOM),
            cost_estimate=pl.CostEstimate(flops=flops, bytes_accessed=0, transcendentals=0),
        )(*args)

    return run


def array(shape, dtype=F32):
    return jax.ShapeDtypeStruct(shape, dtype)


def fold(values):
    rows, width = values.shape
    return jnp.sum((values * values).reshape(rows // 8, 8, width), axis=0)


def local(steps, lines, *refs):
    weights, refs = refs[:3], refs[3:]
    if len(steps) == 1:
        gate, sent, kept, parts, gate_parts, held, gate_held, done, gate_done = refs
    else:
        _, sent, kept, parts, held, done = refs
    line, core = lax.axis_index("zh"), lax.axis_index("c")
    hidden = held.shape[-2]
    copies = []
    for i, step in enumerate(steps):
        first = 2 * lax.rem(line + step, lines)
        for t, weight in enumerate(weights):
            source = weight.at[:, pl.ds(first, 2)]
            copies.append(pltpu.make_async_copy(source, held.at[i, t], done.at[i, t]))
    for copy in copies:
        copy.start()
    if len(steps) == 1:
        gate_copy = pltpu.make_async_copy(gate, gate_held, gate_done)
        gate_copy.start()
    for i in range(len(steps)):
        for t in range(3):
            copies[3 * i + t].wait()
            rows = pl.ds((3 * i + t) * hidden, hidden)
            sent[rows, :] = held[i, t, 0, 1 - core] + held[i, t, 1, 1 - core]
            kept[rows, :] = held[i, t, 0, core] + held[i, t, 1, core]
            for r in range(2):
                for e in range(2):
                    parts[i, r, t, e] = fold(held[i, t, r, e])
    if len(steps) == 1:
        gate_copy.wait()
        end = 3 * hidden * len(steps)
        sent[end : end + 8, :] = gate_held[0] + gate_held[1]
        gate_parts[...] = gate_held[...] * gate_held[...]


def prepare_first(kept, sent, came, message):
    rows = kept.shape[0]
    message[:rows, :] = (kept[...] + came[:rows, :]) * SCALE
    gate = (sent[rows:, :] + came[rows:, :]) * SCALE
    high = gate.astype(jnp.bfloat16).astype(F32)
    message[rows : rows + 8, :] = high
    message[rows + 8 :, :] = gate - high


def prepare_rest(kept, came, far, plus, minus, own):
    rows = own.shape[0]
    for i, message in enumerate((plus, minus)):
        part = pl.ds(i * rows, rows)
        message[:rows, :] = (kept[part, :] + came[part, :]) * SCALE
        message[rows:, :] = far[rows:, :]
    own[...] = (kept[2 * rows :, :] + came[2 * rows :, :]) * SCALE


def count(lines, far_parts, near_parts, gate_parts, small):
    line = lax.axis_index("zh")
    shape = small.shape
    lane = lax.broadcasted_iota(jnp.int32, shape, 1)
    row = lax.broadcasted_iota(jnp.int32, shape, 0)
    total = jnp.zeros(shape, F32)

    def put(total, value, where):
        return jnp.where(where, jnp.broadcast_to(value, shape), total)

    def whole(values):
        return jnp.sum(jnp.sum(values, axis=0, keepdims=True), axis=1, keepdims=True)

    for i, step in enumerate((*STEPS, 0)):
        part = far_parts.at[0] if i == 0 else near_parts.at[i - 1]
        expert = 2 * lax.rem(line + step, lines)
        for r in range(2):
            for t in range(3):
                for e in range(2):
                    total = put(total, whole(part[r, t, e]), (row == r * 4 + t) & (lane == expert + e))
    for r in range(2):
        gate_rows = jnp.sum(gate_parts[r], axis=1, keepdims=True)
        for e in range(8):
            total = put(total, gate_rows[e : e + 1, :], (row == r * 4 + 3) & (lane == e))
    small[...] = total


def combine(peers, lines, own, plus, far, minus, message, counted, out, held):
    line, core = lax.axis_index("zh"), lax.axis_index("c")
    rows, width = own.shape
    hidden = rows // 3
    each = hidden // peers
    factor = 1.0 / (SCALE * lines * 2 * 2)
    soup = (own[...] + far[:rows, :]) + (plus[:rows, :] + minus[:rows, :])
    held[...] = (soup * factor).astype(jnp.bfloat16).astype(F32)
    gates = [
        ref[rows : rows + 8, :] + ref[rows + 8 :, :]
        for ref in (message, far, plus, minus)
    ]
    serve_gate = (((gates[0] + gates[1]) + (gates[2] + gates[3])) * factor).astype(jnp.bfloat16)
    gate = serve_gate.astype(F32)

    lane = lax.broadcasted_iota(jnp.int32, (8, width), 1)
    row = lax.broadcasted_iota(jnp.int32, (8, width), 0)
    small = counted[...]
    for t in range(3):
        total = jnp.sum(fold(held[t * hidden : (t + 1) * hidden, :]), axis=0, keepdims=True)
        total = jnp.broadcast_to(jnp.sum(total, axis=1, keepdims=True), (8, width))
        small = jnp.where((row == 0) & (lane == 16 + t), total, small)
    squares = jnp.broadcast_to(jnp.sum(gate * gate, axis=1, keepdims=True), (8, width))
    small = jnp.where((row == line * 2 + core) & (lane == 19), squares, small)
    high = small.astype(jnp.bfloat16).astype(F32)
    small = (high + pltpu.roll(small - high, width // 2, 1)).astype(jnp.bfloat16)
    for peer in range(peers):
        out[peer, :8, :] = serve_gate
        out[peer, 8:16, :] = small
        for t in range(3):
            start = 16 + t * each
            source = t * hidden + peer * each
            out[peer, start : start + each, :] = held[source : source + each, :].astype(jnp.bfloat16)


def finish(arrived, out1, out3, out2, gate, soup, replica):
    peers, _, width = arrived.shape
    experts = gate.shape[0]
    each = out1.shape[1]
    for peer in range(peers):
        columns = pl.ds(peer * width, width)
        gate[:, columns] = arrived[peer, :experts, :]
        for k, out in enumerate((out1, out3, out2)):
            start = 2 * experts + k * each
            out[0, :, columns] = arrived[peer, start : start + each, :]
    sums = jnp.sum(arrived[:, experts : 2 * experts, :].astype(F32), axis=0)
    sums = sums + pltpu.roll(sums, width // 2, 1)
    over_rows = jnp.sum(sums, axis=0, keepdims=True)
    lane = lax.broadcasted_iota(jnp.int32, sums.shape, 1)
    column = jnp.where(lane < 2 * experts, lax.broadcasted_iota(jnp.int32, sums.shape, 0), lane)
    row_entries = peers * width
    entries = jnp.where(lax.rem(column, 4) == 3, row_entries, peers * each * row_entries)
    sums = jnp.where(lane < 2 * experts, sums, over_rows)
    norms = jnp.sqrt(sums / entries.astype(F32))
    replica[...] = norms[:, :experts]
    soup[...] = pltpu.roll(norms, width - 2 * experts, 1)[:1, :4]


def steps(rep_w1, rep_w3, rep_w2, rep_gate):
    lines = lax.axis_size("zh")
    peers = lax.axis_size(SA)
    held, experts, hidden, width = rep_w1.shape
    each = hidden // peers
    model_width = width * peers
    rows = 3 * hidden
    swap = [(0, 1), (1, 0)]
    rep_w1, rep_w3, rep_w2, rep_gate = (
        pltpu.with_memory_space_constraint(a, pltpu.HBM) for a in (rep_w1, rep_w3, rep_w2, rep_gate)
    )
    weights = (rep_w1, rep_w3, rep_w2)

    def buffers(n):
        return (pltpu.VMEM((n, 3, held, 2, hidden, width), F32),)

    far_sent, far_kept, far_parts, gate_parts = call(
        functools.partial(local, STEPS[:1], lines),
        (array((rows + 8, width)), array((rows, width)), array((1, held, 3, 2, 8, width)), array((held, 8, width))),
        1 << 22,
        buffers(1)
        + (pltpu.VMEM((held, 8, width), F32), pltpu.SemaphoreType.DMA((1, 3)), pltpu.SemaphoreType.DMA),
        in_hbm=4,
    )(*weights, rep_gate)
    far_came = lax.ppermute(far_sent, "c", swap)
    near_sent, near_kept, near_parts = call(
        functools.partial(local, (*STEPS[1:], 0), lines),
        (array((3 * rows, width)), array((3 * rows, width)), array((3, held, 3, 2, 8, width))),
        1 << 23,
        buffers(3) + (pltpu.SemaphoreType.DMA((3, 3)),),
        in_hbm=3,
    )(*weights, gate_parts)
    near_came = lax.ppermute(near_sent, "c", swap)

    def along(message, step):
        pairs = [(i, (i + step) % lines) for i in range(lines)]
        return lax.ppermute(message.astype(jnp.float16), "zh", pairs).astype(F32)

    half = array((rows + 16, width))
    far = call(prepare_first, half, 1 << 20)(far_kept, far_sent, far_came)
    came = {STEPS[0]: along(far, STEPS[0])}
    plus, minus, own = call(prepare_rest, (half, half, array((rows, width))), 1 << 21)(near_kept, near_came, far)
    came[STEPS[1]] = along(plus, STEPS[1])
    came[STEPS[2]] = along(minus, STEPS[2])
    counted = call(functools.partial(count, lines), array((8, width)), 1 << 20)(far_parts, near_parts, gate_parts)
    message = call(
        functools.partial(combine, peers, lines),
        array((peers, 32, width), jnp.bfloat16),
        1 << 22,
        (pltpu.VMEM((rows, width), F32),),
    )(own, came[1], came[2], came[3], far.astype(jnp.float16).astype(F32), counted)
    arrived = lax.all_to_all(message, SA, 0, 0, tiled=True)
    shard = array((1, each, model_width), jnp.bfloat16)
    *served, soup_norms, replica_norms = call(
        finish,
        (
            shard,
            shard,
            shard,
            array((experts, model_width), jnp.bfloat16),
            array((1, 4)),
            array((held * 4, experts)),
        ),
        1 << 20,
    )(arrived)
    replica_norms = replica_norms.reshape(held, 4, experts).transpose(0, 2, 1)
    return (*served, soup_norms, replica_norms)


def solution(mesh):
    torus = Mesh(mesh.devices.reshape(mesh.shape["row"] // 2, 2, 2, 4, 4), ROW + SA)
    in_specs = (
        P(ROW, None, None, SA),
        P(ROW, None, None, SA),
        P(ROW, None, None, SA),
        P(ROW, None, SA),
    )
    out_specs = (
        P(ROW, SA, None),
        P(ROW, SA, None),
        P(ROW, SA, None),
        P(),
        P(ROW, None),
        P(ROW, None, None),
    )
    return jax.shard_map(steps, mesh=torus, in_specs=in_specs, out_specs=out_specs, check_vma=False)
```

profile of v0, /device:TPU:1, one launch (start us, length us, event | category | flops | bytes accessed | tf_op | source)
XLA Modules:
  0.0 40.5 jit_solution(7620962273152086413)
XLA Ops:
  0.6 1.2 %shard_map.91 = (f32[392,128]{1,0:T(8,128)S(1)}, f32[384,128]{1,0:T(8,128)S(1)}, f32[1,2,3,2,8,128]{5,4,3,2,1,0:T(8,128)S(1)}, f32[2,8,128]{2,1,0:T(8,128)S(1)}) custom-call(f32[2,8,128,128]{3,2,1,0:T(8,128)} %refs_0_.3, f32[2,8,128,128]{3,2,1,0:T(8,128)} %refs_1_.3, f32[2,8,128,128]{3,2,1,0:T(8,128)} %refs_2_.3, f32[2,8,128]{2,1,0:T(8,128)} %refs_3_.1), custom_call_target="tpu_custom_call" | custom-call | flops 4194304 | tf_op jit(solution)/shard_map/pallas_call | solution.py:24
  1.8 1.7 %shard_map.92 = (f32[1152,128]{1,0:T(8,128)S(1)}, f32[1152,128]{1,0:T(8,128)S(1)}, f32[3,2,3,2,8,128]{5,4,3,2,1,0:T(8,128)S(1)}) custom-call(f32[2,8,128,128]{3,2,1,0:T(8,128)} %refs_0_.3, f32[2,8,128,128]{3,2,1,0:T(8,128)} %refs_1_.3, f32[2,8,128,128]{3,2,1,0:T(8,128)} %refs_2_.3, f32[2,8,128]{2,1,0:T(8,128)S(1)} %get-tuple-element.22.refs_3_.gate_parts), custom_call_target="tpu_custom_call" | custom-call | flops 8388608 | tf_op jit(solution)/shard_map/pallas_call | solution.py:24
  3.6 3.3 %collective-permute-start = (f32[1152,128]{1,0:T(8,128)S(1)}, f32[1152,128]{1,0:T(8,128)S(1)}, u32[]{:S(2)}, u32[]{:S(2)}) collective-permute-start(f32[1152,128]{1,0:T(8,128)S(1)} %get-tuple-element.24), channel_id=1, source_target_pairs={{0,32},{32,0},{1,33},{33,1},{2,34},{34,2},{3,35},{35,3},{4,36},{36... | collective-permute-start | bytes 1769480 | tf_op jit(solution)/shard_map/ppermute | solution.py:216
  6.9 0.1 collective-permute-start.1
  7.0 1.8 %collective-permute-done.1.came = f32[392,128]{1,0:T(8,128)S(1)} collective-permute-done((f32[392,128]{1,0:T(8,128)S(1)}, f32[392,128]{1,0:T(8,128)S(1)}, u32[]{:S(2)}, u32[]{:S(2)}) %collective-permute-start.1) | collective-permute-done | bytes 200736 | tf_op jit(solution)/shard_map/ppermute | solution.py:208
  8.8 5.3 %collective-permute-start.3 = (f16[400,128]{1,0:T(8,128)(2,1)S(1)}, f16[400,128]{1,0:T(8,128)(2,1)S(1)}, u32[]{:S(2)}, u32[]{:S(2)}) collective-permute-start(f16[400,128]{1,0:T(8,128)(2,1)S(1)} %get-tuple-element.39), channel_id=1, source_target_pairs={{0,128},{64,192},{128,0},{192,64},{1,129},{65,193},{129,1},{193,65... | collective-permute-start | bytes 307208 | tf_op jit(solution)/shard_map/ppermute | solution.py:220
  14.1 0.0 collective-permute-done.came
  14.1 0.1 shard_map.94
  14.2 1.3 %collective-permute-start.2 = (f16[400,128]{1,0:T(8,128)(2,1)S(1)}, f16[400,128]{1,0:T(8,128)(2,1)S(1)}, u32[]{:S(2)}, u32[]{:S(2)}) collective-permute-start(f16[400,128]{1,0:T(8,128)(2,1)S(1)} %convert_element_type.22), channel_id=1, source_target_pairs={{0,64},{64,128},{128,192},{192,0},{1,65},{65,129},{129,193},{193,1... | collective-permute-start | bytes 307208 | tf_op jit(solution)/shard_map/ppermute | solution.py:220
  15.5 2.5 %collective-permute-start.4 = (f16[400,128]{1,0:T(8,128)(2,1)S(1)}, f16[400,128]{1,0:T(8,128)(2,1)S(1)}, u32[]{:S(2)}, u32[]{:S(2)}) collective-permute-start(f16[400,128]{1,0:T(8,128)(2,1)S(1)} %convert_element_type.26), channel_id=1, source_target_pairs={{0,192},{64,0},{128,64},{192,128},{1,193},{65,1},{129,65},{193,129... | collective-permute-start | bytes 307208 | tf_op jit(solution)/shard_map/ppermute | solution.py:220
  18.0 0.1 shard_map.95.counted
  18.1 0.0 collective-permute-done.3
  18.2 2.9 %collective-permute-done.2 = f16[400,128]{1,0:T(8,128)(2,1)S(1)} collective-permute-done((f16[400,128]{1,0:T(8,128)(2,1)S(1)}, f16[400,128]{1,0:T(8,128)(2,1)S(1)}, u32[]{:S(2)}, u32[]{:S(2)}) %collective-permute-start.2) | collective-permute-done | bytes 102432 | tf_op jit(solution)/shard_map/ppermute | solution.py:220
  21.1 3.4 %collective-permute-done.4 = f16[400,128]{1,0:T(8,128)(2,1)S(1)} collective-permute-done((f16[400,128]{1,0:T(8,128)(2,1)S(1)}, f16[400,128]{1,0:T(8,128)(2,1)S(1)}, u32[]{:S(2)}, u32[]{:S(2)}) %collective-permute-start.4) | collective-permute-done | bytes 102432 | tf_op jit(solution)/shard_map/ppermute | solution.py:220
  24.5 0.2 shard_map.96
  24.7 14.9 %all_to_all.5.arrived = bf16[32,32,128]{2,1,0:T(8,128)(2,1)S(1)} all-to-all(bf16[32,32,128]{2,1,0:T(8,128)(2,1)S(1)} %shard_map.96), channel_id=1, replica_groups=mesh['zh'=4,'c'=2,'zl'=2,'x'=4,'y'=4] {'zl','x','y'}, dimensions={0} | all-to-all | bytes 524288 | tf_op jit(solution)/shard_map/all_to_all | solution.py:235
  39.7 0.8 %shard_map.97 = (bf16[1,4,4096]{2,1,0:T(4,128)(2,1)}, bf16[1,4,4096]{2,1,0:T(4,128)(2,1)}, bf16[1,4,4096]{2,1,0:T(4,128)(2,1)}, bf16[8,4096]{1,0:T(8,128)(2,1)}, f32[1,4]{1,0:T(1,128)}, /*index=5*/f32[8,8]{1,0:T(8,128)}) custom-call(bf16[32,32,128]{2,1,0:T(8,128)(2,1)S(1)} %all_to_all.5.arrived), custom_call_target="tpu_custom_call" | custom-call | flops 1048576 | tf_op jit(solution)/shard_map/pallas_call | solution.py:24
  (7 shorter events, 0.1 us)
Async XLA Ops:
  3.6 10.6 %collective-permute-start = (f32[1152,128]{1,0:T(8,128)S(1)}, f32[1152,128]{1,0:T(8,128)S(1)}, u32[]{:S(2)}, u32[]{:S(2)}) collective-permute-start(f32[1152,128]{1,0:T(8,128)S(1)} %get-tuple-element.24), channel_id=1, source_target_pairs={{0,32},{32,0},{1,33},{33,1},{2,34},{34,2},{3,35},{35,3},{4,36},{36... | collective-permute-start | bytes 1769480 | tf_op jit(solution)/shard_map/ppermute | solution.py:216
  6.9 1.9 %collective-permute-start.1 = (f32[392,128]{1,0:T(8,128)S(1)}, f32[392,128]{1,0:T(8,128)S(1)}, u32[]{:S(2)}, u32[]{:S(2)}) collective-permute-start(f32[392,128]{1,0:T(8,128)S(1)} %get-tuple-element.26.sent), channel_id=1, source_target_pairs={{0,32},{32,0},{1,33},{33,1},{2,34},{34,2},{3,35},{35,3},{4,36},{36... | collective-permute-start | bytes 602120 | tf_op jit(solution)/shard_map/ppermute | solution.py:208
  8.8 9.3 %collective-permute-start.3 = (f16[400,128]{1,0:T(8,128)(2,1)S(1)}, f16[400,128]{1,0:T(8,128)(2,1)S(1)}, u32[]{:S(2)}, u32[]{:S(2)}) collective-permute-start(f16[400,128]{1,0:T(8,128)(2,1)S(1)} %get-tuple-element.39), channel_id=1, source_target_pairs={{0,128},{64,192},{128,0},{192,64},{1,129},{65,193},{129,1},{193,65... | collective-permute-start | bytes 307208 | tf_op jit(solution)/shard_map/ppermute | solution.py:220
  14.2 6.8 %collective-permute-start.2 = (f16[400,128]{1,0:T(8,128)(2,1)S(1)}, f16[400,128]{1,0:T(8,128)(2,1)S(1)}, u32[]{:S(2)}, u32[]{:S(2)}) collective-permute-start(f16[400,128]{1,0:T(8,128)(2,1)S(1)} %convert_element_type.22), channel_id=1, source_target_pairs={{0,64},{64,128},{128,192},{192,0},{1,65},{65,129},{129,193},{193,1... | collective-permute-start | bytes 307208 | tf_op jit(solution)/shard_map/ppermute | solution.py:220
  15.5 9.0 %collective-permute-start.4 = (f16[400,128]{1,0:T(8,128)(2,1)S(1)}, f16[400,128]{1,0:T(8,128)(2,1)S(1)}, u32[]{:S(2)}, u32[]{:S(2)}) collective-permute-start(f16[400,128]{1,0:T(8,128)(2,1)S(1)} %convert_element_type.26), channel_id=1, source_target_pairs={{0,192},{64,0},{128,64},{192,128},{1,193},{65,1},{129,65},{193,129... | collective-permute-start | bytes 307208 | tf_op jit(solution)/shard_map/ppermute | solution.py:220
where the time goes:
time: 40.6 us; the launch traced here: 40.5 us
  blocking collectives  14.9 us (37%)
  starting transfers between devices  12.4 us (31%)
  waiting for transfers between devices  8.11 us (20%)
  Pallas kernels  4.18 us (10%)
  between operations  0.71 us (2%)
    all_to_all x1, blocking collectives, steps(): arrived = lax.all_to_all(message, SA, 0, 0, tiled=True)  14.9 us
    ppermute x3, starting transfers between devices, along(): return lax.ppermute(message.astype(jnp.float16), 'zh', pairs).astype(F32)  9.02 us
    ppermute x3, waiting for transfers between devices, along(): return lax.ppermute(message.astype(jnp.float16), 'zh', pairs).astype(F32)  6.29 us
    pallas_call x7, Pallas kernels, run(): pl.pallas_call(kernel, out_shape=out_shape, in_specs=specs, out_specs=jax...  4.18 us
    ppermute x1, starting transfers between devices, steps(): near_came = lax.ppermute(near_sent, 'c', swap)  3.29 us
    ppermute x1, waiting for transfers between devices, steps(): far_came = lax.ppermute(far_sent, 'c', swap)  1.82 us
  transfers between devices with their start and end apart: 5, of which 3 were waited for; matrix products, arithmetic and copies ran while one was open for 0% of the time, Pallas kernels for 1%

commit v1 on v0

--- a/solution.py
+++ b/solution.py
@@ -45,7 +45,7 @@
 
 def local(steps, lines, *refs):
     weights, refs = refs[:3], refs[3:]
-    if len(steps) == 1:
+    if steps == STEPS[:1]:
         gate, sent, kept, parts, gate_parts, held, gate_held, done, gate_done = refs
     else:
         _, sent, kept, parts, held, done = refs
@@ -59,7 +59,7 @@
             copies.append(pltpu.make_async_copy(source, held.at[i, t], done.at[i, t]))
     for copy in copies:
         copy.start()
-    if len(steps) == 1:
+    if steps == STEPS[:1]:
         gate_copy = pltpu.make_async_copy(gate, gate_held, gate_done)
         gate_copy.start()
     for i in range(len(steps)):
@@ -71,7 +71,7 @@
             for r in range(2):
                 for e in range(2):
                     parts[i, r, t, e] = fold(held[i, t, r, e])
-    if len(steps) == 1:
+    if steps == STEPS[:1]:
         gate_copy.wait()
         end = 3 * hidden * len(steps)
         sent[end : end + 8, :] = gate_held[0] + gate_held[1]
@@ -87,16 +87,15 @@
     message[rows + 8 :, :] = gate - high
 
 
-def prepare_rest(kept, came, far, plus, minus, own):
-    rows = own.shape[0]
+def prepare_rest(kept, came, far, plus, minus):
+    rows = kept.shape[0] // 2
     for i, message in enumerate((plus, minus)):
         part = pl.ds(i * rows, rows)
         message[:rows, :] = (kept[part, :] + came[part, :]) * SCALE
         message[rows:, :] = far[rows:, :]
-    own[...] = (kept[2 * rows :, :] + came[2 * rows :, :]) * SCALE
-
-
-def count(lines, far_parts, near_parts, gate_parts, small):
+
+
+def count(lines, far_parts, near_parts, own_parts, gate_parts, small):
     line = lax.axis_index("zh")
     shape = small.shape
     lane = lax.broadcasted_iota(jnp.int32, shape, 1)
@@ -110,7 +109,7 @@
         return jnp.sum(jnp.sum(values, axis=0, keepdims=True), axis=1, keepdims=True)
 
     for i, step in enumerate((*STEPS, 0)):
-        part = far_parts.at[0] if i == 0 else near_parts.at[i - 1]
+        part = (far_parts.at[0], near_parts.at[0], near_parts.at[1], own_parts.at[0])[i]
         expert = 2 * lax.rem(line + step, lines)
         for r in range(2):
             for t in range(3):
@@ -123,13 +122,14 @@
     small[...] = total
 
 
-def combine(peers, lines, own, plus, far, minus, message, counted, out, held):
+def combine(peers, lines, kept, other, plus, far, minus, message, counted, out, held):
     line, core = lax.axis_index("zh"), lax.axis_index("c")
-    rows, width = own.shape
+    rows, width = kept.shape
     hidden = rows // 3
     each = hidden // peers
     factor = 1.0 / (SCALE * lines * 2 * 2)
-    soup = (own[...] + far[:rows, :]) + (plus[:rows, :] + minus[:rows, :])
+    own = (kept[...] + other[...]) * SCALE
+    soup = (own + far[:rows, :]) + (plus[:rows, :] + minus[:rows, :])
     held[...] = (soup * factor).astype(jnp.bfloat16).astype(F32)
     gates = [
         ref[rows : rows + 8, :] + ref[rows + 8 :, :]
@@ -207,13 +207,21 @@
     )(*weights, rep_gate)
     far_came = lax.ppermute(far_sent, "c", swap)
     near_sent, near_kept, near_parts = call(
-        functools.partial(local, (*STEPS[1:], 0), lines),
-        (array((3 * rows, width)), array((3 * rows, width)), array((3, held, 3, 2, 8, width))),
+        functools.partial(local, STEPS[1:], lines),
+        (array((2 * rows, width)), array((2 * rows, width)), array((2, held, 3, 2, 8, width))),
         1 << 23,
-        buffers(3) + (pltpu.SemaphoreType.DMA((3, 3)),),
+        buffers(2) + (pltpu.SemaphoreType.DMA((2, 3)),),
         in_hbm=3,
     )(*weights, gate_parts)
     near_came = lax.ppermute(near_sent, "c", swap)
+    own_sent, own_kept, own_parts = call(
+        functools.partial(local, (0,), lines),
+        (array((rows, width)), array((rows, width)), array((1, held, 3, 2, 8, width))),
+        1 << 22,
+        buffers(1) + (pltpu.SemaphoreType.DMA((1, 3)),),
+        in_hbm=3,
+    )(*weights, gate_parts)
+    own_came = lax.ppermute(own_sent, "c", swap)
 
     def along(message, step):
         pairs = [(i, (i + step) % lines) for i in range(lines)]
@@ -222,16 +230,20 @@
     half = array((rows + 16, width))
     far = call(prepare_first, half, 1 << 20)(far_kept, far_sent, far_came)
     came = {STEPS[0]: along(far, STEPS[0])}
-    plus, minus, own = call(prepare_rest, (half, half, array((rows, width))), 1 << 21)(near_kept, near_came, far)
+    plus, minus = call(prepare_rest, (half, half), 1 << 21)(
+        near_kept, near_came, far
+    )
     came[STEPS[1]] = along(plus, STEPS[1])
     came[STEPS[2]] = along(minus, STEPS[2])
-    counted = call(functools.partial(count, lines), array((8, width)), 1 << 20)(far_parts, near_parts, gate_parts)
+    counted = call(functools.partial(count, lines), array((8, width)), 1 << 20)(
+        far_parts, near_parts, own_parts, gate_parts
+    )
     message = call(
         functools.partial(combine, peers, lines),
         array((peers, 32, width), jnp.bfloat16),
         1 << 22,
         (pltpu.VMEM((rows, width), F32),),
-    )(own, came[1], came[2], came[3], far.astype(jnp.float16).astype(F32), counted)
+    )(own_kept, own_came, came[1], came[2], came[3], far.astype(jnp.float16).astype(F32), counted)
     arrived = lax.all_to_all(message, SA, 0, 0, tiled=True)
     shard = array((1, each, model_width), jnp.bfloat16)
     *served, soup_norms, replica_norms = call(

time: 40.6 us -> 40.4 us (level)
  waiting for transfers between devices: 8.11 us -> 6.44 us
  Pallas kernels: 4.18 us -> 5.07 us
  starting transfers between devices: 12.4 us -> 13 us
    ppermute x1, starting transfers between devices: 0.1 us -> 3.29 us  [steps(): far_came = lax.ppermute(far_sent, 'c', swap)]
    ppermute x1, starting transfers between devices: 3.29 us -> 0.12 us  [steps(): near_came = lax.ppermute(near_sent, 'c', swap)]
    ppermute x1, waiting for transfers between devices: 1.82 us -> 0.01 us  [steps(): far_came = lax.ppermute(far_sent, 'c', swap)]
    pallas_call x7 -> x8, Pallas kernels: 4.18 us -> 5.07 us  [run(): pl.pallas_call(kernel, out_shape=out_shape, in_specs=specs, out_specs=jax...]
    ppermute x0 -> x1, starting transfers between devices: none -> 0.57 us  [steps(): own_came = lax.ppermute(own_sent, 'c', swap)]
  transfers between devices with their start and end apart: 5 -> 6, of which waited for: 3 -> 2; matrix products, arithmetic and copies ran while one was open for 0% -> 0% of each run, Pallas kernels for 1% -> 7%
where the time goes in v1:
time: 40.4 us; the launch traced here: 40.2 us
  blocking collectives  14.9 us (37%)
  starting transfers between devices  13 us (32%)
  waiting for transfers between devices  6.44 us (16%)
  Pallas kernels  5.07 us (13%)
  between operations  0.73 us (2%)
    all_to_all x1, blocking collectives, steps(): arrived = lax.all_to_all(message, SA, 0, 0, tiled=True)  14.9 us
    ppermute x3, starting transfers between devices, along(): return lax.ppermute(message.astype(jnp.float16), 'zh', pairs).astype(F32)  9.02 us
    ppermute x3, waiting for transfers between devices, along(): return lax.ppermute(message.astype(jnp.float16), 'zh', pairs).astype(F32)  6.43 us
    pallas_call x8, Pallas kernels, run(): pl.pallas_call(kernel, out_shape=out_shape, in_specs=specs, out_specs=jax...  5.07 us
    ppermute x1, starting transfers between devices, steps(): far_came = lax.ppermute(far_sent, 'c', swap)  3.29 us
  transfers between devices with their start and end apart: 6, of which 2 were waited for; matrix products, arithmetic and copies ran while one was open for 0% of the time, Pallas kernels for 7%

profile of v1, /device:TPU:1, one launch (start us, length us, event | category | flops | bytes accessed | tf_op | source)
XLA Modules:
  0.0 40.2 jit_solution(13596541363041056965)
XLA Ops:
  0.6 1.2 %shard_map.91 = (f32[392,128]{1,0:T(8,128)S(1)}, f32[384,128]{1,0:T(8,128)S(1)}, f32[1,2,3,2,8,128]{5,4,3,2,1,0:T(8,128)S(1)}, f32[2,8,128]{2,1,0:T(8,128)S(1)}) custom-call(f32[2,8,128,128]{3,2,1,0:T(8,128)} %refs_0_.5, f32[2,8,128,128]{3,2,1,0:T(8,128)} %refs_1_.5, f32[2,8,128,128]{3,2,1,0:T(8,128)} %refs_2_.5, f32[2,8,128]{2,1,0:T(8,128)} %refs_3_.1), custom_call_target="tpu_custom_call" | custom-call | flops 4194304 | tf_op jit(solution)/shard_map/pallas_call | solution.py:24
  1.8 3.3 %collective-permute-start.2 = (f32[392,128]{1,0:T(8,128)S(1)}, f32[392,128]{1,0:T(8,128)S(1)}, u32[]{:S(2)}, u32[]{:S(2)}) collective-permute-start(f32[392,128]{1,0:T(8,128)S(1)} %get-tuple-element.30.sent), channel_id=1, source_target_pairs={{0,32},{32,0},{1,33},{33,1},{2,34},{34,2},{3,35},{35,3},{4,36},{36... | collective-permute-start | bytes 602120 | tf_op jit(solution)/shard_map/ppermute | solution.py:208
  5.1 1.4 %shard_map.93 = (f32[768,128]{1,0:T(8,128)S(1)}, f32[768,128]{1,0:T(8,128)S(1)}, f32[2,2,3,2,8,128]{5,4,3,2,1,0:T(8,128)S(1)}) custom-call(f32[2,8,128,128]{3,2,1,0:T(8,128)} %refs_0_.5, f32[2,8,128,128]{3,2,1,0:T(8,128)} %refs_1_.5, f32[2,8,128,128]{3,2,1,0:T(8,128)} %refs_2_.5, f32[2,8,128]{2,1,0:T(8,128)S(1)} %get-tuple-element.24.refs_3_.gate_parts), custom_call_target="tpu_custom_call" | custom-call | flops 8388608 | tf_op jit(solution)/shard_map/pallas_call | solution.py:24
  6.6 0.1 collective-permute-start.1
  6.7 1.2 %shard_map.92 = (f32[384,128]{1,0:T(8,128)S(1)}, f32[384,128]{1,0:T(8,128)S(1)}, f32[1,2,3,2,8,128]{5,4,3,2,1,0:T(8,128)S(1)}) custom-call(f32[2,8,128,128]{3,2,1,0:T(8,128)} %refs_0_.5, f32[2,8,128,128]{3,2,1,0:T(8,128)} %refs_1_.5, f32[2,8,128,128]{3,2,1,0:T(8,128)} %refs_2_.5, f32[2,8,128]{2,1,0:T(8,128)S(1)} %get-tuple-element.24.refs_3_.gate_parts), custom_call_target="tpu_custom_call" | custom-call | flops 4194304 | tf_op jit(solution)/shard_map/pallas_call | solution.py:24
  7.9 0.6 %collective-permute-start = (f32[384,128]{1,0:T(8,128)S(1)}, f32[384,128]{1,0:T(8,128)S(1)}, u32[]{:S(2)}, u32[]{:S(2)}) collective-permute-start(f32[384,128]{1,0:T(8,128)S(1)} %get-tuple-element.26), channel_id=1, source_target_pairs={{0,32},{32,0},{1,33},{33,1},{2,34},{34,2},{3,35},{35,3},{4,36},{36... | collective-permute-start | bytes 589832 | tf_op jit(solution)/shard_map/ppermute | solution.py:224
  8.4 0.0 collective-permute-done.2.came
  8.5 5.3 %collective-permute-start.4 = (f16[400,128]{1,0:T(8,128)(2,1)S(1)}, f16[400,128]{1,0:T(8,128)(2,1)S(1)}, u32[]{:S(2)}, u32[]{:S(2)}) collective-permute-start(f16[400,128]{1,0:T(8,128)(2,1)S(1)} %get-tuple-element.43), channel_id=1, source_target_pairs={{0,128},{64,192},{128,0},{192,64},{1,129},{65,193},{129,1},{193,65... | collective-permute-start | bytes 307208 | tf_op jit(solution)/shard_map/ppermute | solution.py:228
  13.8 0.0 collective-permute-done.1.came
  13.8 0.1 shard_map.95
  13.9 1.3 %collective-permute-start.3 = (f16[400,128]{1,0:T(8,128)(2,1)S(1)}, f16[400,128]{1,0:T(8,128)(2,1)S(1)}, u32[]{:S(2)}, u32[]{:S(2)}) collective-permute-start(f16[400,128]{1,0:T(8,128)(2,1)S(1)} %convert_element_type.22), channel_id=1, source_target_pairs={{0,64},{64,128},{128,192},{192,0},{1,65},{65,129},{129,193},{193,1... | collective-permute-start | bytes 307208 | tf_op jit(solution)/shard_map/ppermute | solution.py:228
  15.2 2.5 %collective-permute-start.5 = (f16[400,128]{1,0:T(8,128)(2,1)S(1)}, f16[400,128]{1,0:T(8,128)(2,1)S(1)}, u32[]{:S(2)}, u32[]{:S(2)}) collective-permute-start(f16[400,128]{1,0:T(8,128)(2,1)S(1)} %convert_element_type.26), channel_id=1, source_target_pairs={{0,192},{64,0},{128,64},{192,128},{1,193},{65,1},{129,65},{193,129... | collective-permute-start | bytes 307208 | tf_op jit(solution)/shard_map/ppermute | solution.py:228
  17.6 0.1 shard_map.96.counted
  17.8 0.0 collective-permute-done.4
  17.8 3.3 %collective-permute-done.3 = f16[400,128]{1,0:T(8,128)(2,1)S(1)} collective-permute-done((f16[400,128]{1,0:T(8,128)(2,1)S(1)}, f16[400,128]{1,0:T(8,128)(2,1)S(1)}, u32[]{:S(2)}, u32[]{:S(2)}) %collective-permute-start.3) | collective-permute-done | bytes 102432 | tf_op jit(solution)/shard_map/ppermute | solution.py:228
  21.1 3.2 %collective-permute-done.5 = f16[400,128]{1,0:T(8,128)(2,1)S(1)} collective-permute-done((f16[400,128]{1,0:T(8,128)(2,1)S(1)}, f16[400,128]{1,0:T(8,128)(2,1)S(1)}, u32[]{:S(2)}, u32[]{:S(2)}) %collective-permute-start.5) | collective-permute-done | bytes 102432 | tf_op jit(solution)/shard_map/ppermute | solution.py:228
  24.3 0.0 collective-permute-done.other
  24.3 0.3 shard_map.97
  24.6 14.9 %all_to_all.5.arrived = bf16[32,32,128]{2,1,0:T(8,128)(2,1)S(1)} all-to-all(bf16[32,32,128]{2,1,0:T(8,128)(2,1)S(1)} %shard_map.97), channel_id=1, replica_groups=mesh['zh'=4,'c'=2,'zl'=2,'x'=4,'y'=4] {'zl','x','y'}, dimensions={0} | all-to-all | bytes 524288 | tf_op jit(solution)/shard_map/all_to_all | solution.py:247
  39.4 0.8 %shard_map.98 = (bf16[1,4,4096]{2,1,0:T(4,128)(2,1)}, bf16[1,4,4096]{2,1,0:T(4,128)(2,1)}, bf16[1,4,4096]{2,1,0:T(4,128)(2,1)}, bf16[8,4096]{1,0:T(8,128)(2,1)}, f32[1,4]{1,0:T(1,128)}, /*index=5*/f32[8,8]{1,0:T(8,128)}) custom-call(bf16[32,32,128]{2,1,0:T(8,128)(2,1)S(1)} %all_to_all.5.arrived), custom_call_target="tpu_custom_call" | custom-call | flops 1048576 | tf_op jit(solution)/shard_map/pallas_call | solution.py:24
  (7 shorter events, 0.1 us)
Async XLA Ops:
  1.8 6.6 %collective-permute-start.2 = (f32[392,128]{1,0:T(8,128)S(1)}, f32[392,128]{1,0:T(8,128)S(1)}, u32[]{:S(2)}, u32[]{:S(2)}) collective-permute-start(f32[392,128]{1,0:T(8,128)S(1)} %get-tuple-element.30.sent), channel_id=1, source_target_pairs={{0,32},{32,0},{1,33},{33,1},{2,34},{34,2},{3,35},{35,3},{4,36},{36... | collective-permute-start | bytes 602120 | tf_op jit(solution)/shard_map/ppermute | solution.py:208
  6.6 7.2 %collective-permute-start.1 = (f32[768,128]{1,0:T(8,128)S(1)}, f32[768,128]{1,0:T(8,128)S(1)}, u32[]{:S(2)}, u32[]{:S(2)}) collective-permute-start(f32[768,128]{1,0:T(8,128)S(1)} %get-tuple-element.28), channel_id=1, source_target_pairs={{0,32},{32,0},{1,33},{33,1},{2,34},{34,2},{3,35},{35,3},{4,36},{36... | collective-permute-start | bytes 1179656 | tf_op jit(solution)/shard_map/ppermute | solution.py:216
  7.9 16.4 %collective-permute-start = (f32[384,128]{1,0:T(8,128)S(1)}, f32[384,128]{1,0:T(8,128)S(1)}, u32[]{:S(2)}, u32[]{:S(2)}) collective-permute-start(f32[384,128]{1,0:T(8,128)S(1)} %get-tuple-element.26), channel_id=1, source_target_pairs={{0,32},{32,0},{1,33},{33,1},{2,34},{34,2},{3,35},{35,3},{4,36},{36... | collective-permute-start | bytes 589832 | tf_op jit(solution)/shard_map/ppermute | solution.py:224
  8.5 9.3 %collective-permute-start.4 = (f16[400,128]{1,0:T(8,128)(2,1)S(1)}, f16[400,128]{1,0:T(8,128)(2,1)S(1)}, u32[]{:S(2)}, u32[]{:S(2)}) collective-permute-start(f16[400,128]{1,0:T(8,128)(2,1)S(1)} %get-tuple-element.43), channel_id=1, source_target_pairs={{0,128},{64,192},{128,0},{192,64},{1,129},{65,193},{129,1},{193,65... | collective-permute-start | bytes 307208 | tf_op jit(solution)/shard_map/ppermute | solution.py:228
  13.9 7.2 %collective-permute-start.3 = (f16[400,128]{1,0:T(8,128)(2,1)S(1)}, f16[400,128]{1,0:T(8,128)(2,1)S(1)}, u32[]{:S(2)}, u32[]{:S(2)}) collective-permute-start(f16[400,128]{1,0:T(8,128)(2,1)S(1)} %convert_element_type.22), channel_id=1, source_target_pairs={{0,64},{64,128},{128,192},{192,0},{1,65},{65,129},{129,193},{193,1... | collective-permute-start | bytes 307208 | tf_op jit(solution)/shard_map/ppermute | solution.py:228
  15.2 9.1 %collective-permute-start.5 = (f16[400,128]{1,0:T(8,128)(2,1)S(1)}, f16[400,128]{1,0:T(8,128)(2,1)S(1)}, u32[]{:S(2)}, u32[]{:S(2)}) collective-permute-start(f16[400,128]{1,0:T(8,128)(2,1)S(1)} %convert_element_type.26), channel_id=1, source_target_pairs={{0,192},{64,0},{128,64},{192,128},{1,193},{65,1},{129,65},{193,129... | collective-permute-start | bytes 307208 | tf_op jit(solution)/shard_map/ppermute | solution.py:228

commit v2 on v1

--- a/solution.py
+++ b/solution.py
@@ -11,7 +11,9 @@
 
 ROW = ("zh", "c")
 SA = ("zl", "x", "y")
-SCALE = 2048.0
+FULL = 32768.0
+LEAST = 2.0**-100
+TINY = 2.0**-30
 STEPS = (2, 1, 3)
 ROOM = 6 << 20
 F32 = jnp.float32
@@ -78,21 +80,53 @@
         gate_parts[...] = gate_held[...] * gate_held[...]
 
 
-def prepare_first(kept, sent, came, message):
-    rows = kept.shape[0]
-    message[:rows, :] = (kept[...] + came[:rows, :]) * SCALE
-    gate = (sent[rows:, :] + came[rows:, :]) * SCALE
-    high = gate.astype(jnp.bfloat16).astype(F32)
-    message[rows : rows + 8, :] = high
-    message[rows + 8 :, :] = gate - high
+def encode(values):
+    top = jnp.max(jnp.abs(values), axis=0, keepdims=True)
+    power = jnp.ceil(jnp.log2(jnp.maximum(top, LEAST)))
+    parts = values * jnp.exp2(-power)
+    return parts * jnp.abs(parts) * FULL, power
+
+
+def decode(codes, power):
+    roots = codes * lax.rsqrt(jnp.maximum(jnp.abs(codes), TINY))
+    return roots * (jnp.exp2(power) * (FULL**-0.5))
+
+
+def write(message, blocks):
+    powers = []
+    rows = 0
+    for block in blocks:
+        codes, power = encode(block)
+        message[rows : rows + block.shape[0], :] = codes
+        rows += block.shape[0]
+        powers.append(power)
+    rest = jnp.zeros((8 - len(powers), powers[0].shape[1]), F32)
+    message[rows:, :] = jnp.concatenate([*powers, rest])
+
+
+def read(message, block):
+    rows, _ = message.shape
+    hidden = (rows - 16) // 3
+    codes = message[rows - 16 : rows - 8, :] if block == 3 else message[block * hidden : (block + 1) * hidden, :]
+    return decode(codes, message[rows - 8 + block : rows - 7 + block, :])
+
+
+def prepare_first(kept, sent, came, message, gate):
+    rows, _ = kept.shape
+    hidden = rows // 3
+    parts = [slice(t * hidden, (t + 1) * hidden) for t in range(3)]
+    blocks = [kept[part, :] + came[part, :] for part in parts]
+    gate[...] = sent[rows:, :] + came[rows:, :]
+    write(message, [*blocks, sent[rows:, :] + came[rows:, :]])
 
 
 def prepare_rest(kept, came, far, plus, minus):
     rows = kept.shape[0] // 2
+    hidden = rows // 3
     for i, message in enumerate((plus, minus)):
-        part = pl.ds(i * rows, rows)
-        message[:rows, :] = (kept[part, :] + came[part, :]) * SCALE
-        message[rows:, :] = far[rows:, :]
+        parts = [slice(i * rows + t * hidden, i * rows + (t + 1) * hidden) for t in range(3)]
+        blocks = [kept[part, :] + came[part, :] for part in parts]
+        write(message, blocks + [far[...]])
 
 
 def count(lines, far_parts, near_parts, own_parts, gate_parts, small):
@@ -127,14 +161,13 @@
     rows, width = kept.shape
     hidden = rows // 3
     each = hidden // peers
-    factor = 1.0 / (SCALE * lines * 2 * 2)
-    own = (kept[...] + other[...]) * SCALE
-    soup = (own + far[:rows, :]) + (plus[:rows, :] + minus[:rows, :])
-    held[...] = (soup * factor).astype(jnp.bfloat16).astype(F32)
-    gates = [
-        ref[rows : rows + 8, :] + ref[rows + 8 :, :]
-        for ref in (message, far, plus, minus)
-    ]
+    factor = 1.0 / (lines * 2 * 2)
+    for t in range(3):
+        part = pl.ds(t * hidden, hidden)
+        soup = kept[part, :] + other[part, :]
+        soup = (soup + read(far, t)) + (read(plus, t) + read(minus, t))
+        held[part, :] = (soup * factor).astype(jnp.bfloat16).astype(F32)
+    gates = [read(ref, 3) for ref in (message, far, plus, minus)]
     serve_gate = (((gates[0] + gates[1]) + (gates[2] + gates[3])) * factor).astype(jnp.bfloat16)
     gate = serve_gate.astype(F32)
 
@@ -228,10 +261,10 @@
         return lax.ppermute(message.astype(jnp.float16), "zh", pairs).astype(F32)
 
     half = array((rows + 16, width))
-    far = call(prepare_first, half, 1 << 20)(far_kept, far_sent, far_came)
+    far, gate = call(prepare_first, (half, array((8, width))), 1 << 20)(far_kept, far_sent, far_came)
     came = {STEPS[0]: along(far, STEPS[0])}
     plus, minus = call(prepare_rest, (half, half), 1 << 21)(
-        near_kept, near_came, far
+        near_kept, near_came, gate
     )
     came[STEPS[1]] = along(plus, STEPS[1])
     came[STEPS[2]] = along(minus, STEPS[2])

time: 40.4 us -> 40.6 us (level)
  no operation moved by 1% of the time
where the time goes in v2:
time: 40.6 us; the launch traced here: 40.4 us
  blocking collectives  14.9 us (37%)
  starting transfers between devices  13 us (32%)
  waiting for transfers between devices  6.37 us (16%)
  Pallas kernels  5.28 us (13%)
  between operations  0.74 us (2%)
    all_to_all x1, blocking collectives, steps(): arrived = lax.all_to_all(message, SA, 0, 0, tiled=True)  14.9 us
    ppermute x3, starting transfers between devices, along(): return lax.ppermute(message.astype(jnp.float16), 'zh', pairs).astype(F32)  9.02 us
    ppermute x3, waiting for transfers between devices, along(): return lax.ppermute(message.astype(jnp.float16), 'zh', pairs).astype(F32)  6.36 us
    pallas_call x8, Pallas kernels, run(): pl.pallas_call(kernel, out_shape=out_shape, in_specs=specs, out_specs=jax...  5.28 us
    ppermute x1, starting transfers between devices, steps(): far_came = lax.ppermute(far_sent, 'c', swap)  3.29 us
  transfers between devices with their start and end apart: 6, of which 2 were waited for; matrix products, arithmetic and copies ran while one was open for 0% of the time, Pallas kernels for 7%

profile of v2, /device:TPU:1, one launch (start us, length us, event | category | flops | bytes accessed | tf_op | source)
XLA Modules:
  0.0 40.4 jit_solution(2047599432849592205)
XLA Ops:
  0.6 1.2 %shard_map.91 = (f32[392,128]{1,0:T(8,128)S(1)}, f32[384,128]{1,0:T(8,128)S(1)}, f32[1,2,3,2,8,128]{5,4,3,2,1,0:T(8,128)S(1)}, f32[2,8,128]{2,1,0:T(8,128)S(1)}) custom-call(f32[2,8,128,128]{3,2,1,0:T(8,128)} %refs_0_.5, f32[2,8,128,128]{3,2,1,0:T(8,128)} %refs_1_.5, f32[2,8,128,128]{3,2,1,0:T(8,128)} %refs_2_.5, f32[2,8,128]{2,1,0:T(8,128)} %refs_3_.1), custom_call_target="tpu_custom_call" | custom-call | flops 4194304 | tf_op jit(solution)/shard_map/pallas_call | solution.py:26
  1.8 3.3 %collective-permute-start.2 = (f32[392,128]{1,0:T(8,128)S(1)}, f32[392,128]{1,0:T(8,128)S(1)}, u32[]{:S(2)}, u32[]{:S(2)}) collective-permute-start(f32[392,128]{1,0:T(8,128)S(1)} %get-tuple-element.32.sent), channel_id=1, source_target_pairs={{0,32},{32,0},{1,33},{33,1},{2,34},{34,2},{3,35},{35,3},{4,36},{36... | collective-permute-start | bytes 602120 | tf_op jit(solution)/shard_map/ppermute | solution.py:241
  5.1 1.4 %shard_map.93 = (f32[768,128]{1,0:T(8,128)S(1)}, f32[768,128]{1,0:T(8,128)S(1)}, f32[2,2,3,2,8,128]{5,4,3,2,1,0:T(8,128)S(1)}) custom-call(f32[2,8,128,128]{3,2,1,0:T(8,128)} %refs_0_.5, f32[2,8,128,128]{3,2,1,0:T(8,128)} %refs_1_.5, f32[2,8,128,128]{3,2,1,0:T(8,128)} %refs_2_.5, f32[2,8,128]{2,1,0:T(8,128)S(1)} %get-tuple-element.26.refs_3_.gate_parts), custom_call_target="tpu_custom_call" | custom-call | flops 8388608 | tf_op jit(solution)/shard_map/pallas_call | solution.py:26
  6.6 0.1 collective-permute-start.1
  6.7 1.2 %shard_map.92 = (f32[384,128]{1,0:T(8,128)S(1)}, f32[384,128]{1,0:T(8,128)S(1)}, f32[1,2,3,2,8,128]{5,4,3,2,1,0:T(8,128)S(1)}) custom-call(f32[2,8,128,128]{3,2,1,0:T(8,128)} %refs_0_.5, f32[2,8,128,128]{3,2,1,0:T(8,128)} %refs_1_.5, f32[2,8,128,128]{3,2,1,0:T(8,128)} %refs_2_.5, f32[2,8,128]{2,1,0:T(8,128)S(1)} %get-tuple-element.26.refs_3_.gate_parts), custom_call_target="tpu_custom_call" | custom-call | flops 4194304 | tf_op jit(solution)/shard_map/pallas_call | solution.py:26
  7.9 0.6 %collective-permute-start = (f32[384,128]{1,0:T(8,128)S(1)}, f32[384,128]{1,0:T(8,128)S(1)}, u32[]{:S(2)}, u32[]{:S(2)}) collective-permute-start(f32[384,128]{1,0:T(8,128)S(1)} %get-tuple-element.28), channel_id=1, source_target_pairs={{0,32},{32,0},{1,33},{33,1},{2,34},{34,2},{3,35},{35,3},{4,36},{36... | collective-permute-start | bytes 589832 | tf_op jit(solution)/shard_map/ppermute | solution.py:257
  8.4 0.0 collective-permute-done.2.came
  8.4 0.1 shard_map.94
  8.6 5.3 %collective-permute-start.4 = (f16[400,128]{1,0:T(8,128)(2,1)S(1)}, f16[400,128]{1,0:T(8,128)(2,1)S(1)}, u32[]{:S(2)}, u32[]{:S(2)}) collective-permute-start(f16[400,128]{1,0:T(8,128)(2,1)S(1)} %get-tuple-element.47), channel_id=1, source_target_pairs={{0,128},{64,192},{128,0},{192,64},{1,129},{65,193},{129,1},{193,65... | collective-permute-start | bytes 307208 | tf_op jit(solution)/shard_map/ppermute | solution.py:261
  13.8 0.0 collective-permute-done.1.came
  13.8 0.1 shard_map.95
  14.0 1.3 %collective-permute-start.3 = (f16[400,128]{1,0:T(8,128)(2,1)S(1)}, f16[400,128]{1,0:T(8,128)(2,1)S(1)}, u32[]{:S(2)}, u32[]{:S(2)}) collective-permute-start(f16[400,128]{1,0:T(8,128)(2,1)S(1)} %convert_element_type.22), channel_id=1, source_target_pairs={{0,64},{64,128},{128,192},{192,0},{1,65},{65,129},{129,193},{193,1... | collective-permute-start | bytes 307208 | tf_op jit(solution)/shard_map/ppermute | solution.py:261
  15.3 2.5 %collective-permute-start.5 = (f16[400,128]{1,0:T(8,128)(2,1)S(1)}, f16[400,128]{1,0:T(8,128)(2,1)S(1)}, u32[]{:S(2)}, u32[]{:S(2)}) collective-permute-start(f16[400,128]{1,0:T(8,128)(2,1)S(1)} %convert_element_type.26), channel_id=1, source_target_pairs={{0,192},{64,0},{128,64},{192,128},{1,193},{65,1},{129,65},{193,129... | collective-permute-start | bytes 307208 | tf_op jit(solution)/shard_map/ppermute | solution.py:261
  17.7 0.1 shard_map.96.counted
  17.9 0.0 collective-permute-done.4
  17.9 3.0 %collective-permute-done.3 = f16[400,128]{1,0:T(8,128)(2,1)S(1)} collective-permute-done((f16[400,128]{1,0:T(8,128)(2,1)S(1)}, f16[400,128]{1,0:T(8,128)(2,1)S(1)}, u32[]{:S(2)}, u32[]{:S(2)}) %collective-permute-start.3) | collective-permute-done | bytes 102432 | tf_op jit(solution)/shard_map/ppermute | solution.py:261
  20.9 3.4 %collective-permute-done.5 = f16[400,128]{1,0:T(8,128)(2,1)S(1)} collective-permute-done((f16[400,128]{1,0:T(8,128)(2,1)S(1)}, f16[400,128]{1,0:T(8,128)(2,1)S(1)}, u32[]{:S(2)}, u32[]{:S(2)}) %collective-permute-start.5) | collective-permute-done | bytes 102432 | tf_op jit(solution)/shard_map/ppermute | solution.py:261
  24.3 0.0 collective-permute-done.other
  24.3 0.4 shard_map.97
  24.7 14.9 %all_to_all.5.arrived = bf16[32,32,128]{2,1,0:T(8,128)(2,1)S(1)} all-to-all(bf16[32,32,128]{2,1,0:T(8,128)(2,1)S(1)} %shard_map.97), channel_id=1, replica_groups=mesh['zh'=4,'c'=2,'zl'=2,'x'=4,'y'=4] {'zl','x','y'}, dimensions={0} | all-to-all | bytes 524288 | tf_op jit(solution)/shard_map/all_to_all | solution.py:280
  39.6 0.8 %shard_map.98 = (bf16[1,4,4096]{2,1,0:T(4,128)(2,1)}, bf16[1,4,4096]{2,1,0:T(4,128)(2,1)}, bf16[1,4,4096]{2,1,0:T(4,128)(2,1)}, bf16[8,4096]{1,0:T(8,128)(2,1)}, f32[1,4]{1,0:T(1,128)}, /*index=5*/f32[8,8]{1,0:T(8,128)}) custom-call(bf16[32,32,128]{2,1,0:T(8,128)(2,1)S(1)} %all_to_all.5.arrived), custom_call_target="tpu_custom_call" | custom-call | flops 1048576 | tf_op jit(solution)/shard_map/pallas_call | solution.py:26
  (6 shorter events, 0.1 us)
Async XLA Ops:
  1.8 6.6 %collective-permute-start.2 = (f32[392,128]{1,0:T(8,128)S(1)}, f32[392,128]{1,0:T(8,128)S(1)}, u32[]{:S(2)}, u32[]{:S(2)}) collective-permute-start(f32[392,128]{1,0:T(8,128)S(1)} %get-tuple-element.32.sent), channel_id=1, source_target_pairs={{0,32},{32,0},{1,33},{33,1},{2,34},{34,2},{3,35},{35,3},{4,36},{36... | collective-permute-start | bytes 602120 | tf_op jit(solution)/shard_map/ppermute | solution.py:241
  6.6 7.3 %collective-permute-start.1 = (f32[768,128]{1,0:T(8,128)S(1)}, f32[768,128]{1,0:T(8,128)S(1)}, u32[]{:S(2)}, u32[]{:S(2)}) collective-permute-start(f32[768,128]{1,0:T(8,128)S(1)} %get-tuple-element.30), channel_id=1, source_target_pairs={{0,32},{32,0},{1,33},{33,1},{2,34},{34,2},{3,35},{35,3},{4,36},{36... | collective-permute-start | bytes 1179656 | tf_op jit(solution)/shard_map/ppermute | solution.py:249
  7.9 16.5 %collective-permute-start = (f32[384,128]{1,0:T(8,128)S(1)}, f32[384,128]{1,0:T(8,128)S(1)}, u32[]{:S(2)}, u32[]{:S(2)}) collective-permute-start(f32[384,128]{1,0:T(8,128)S(1)} %get-tuple-element.28), channel_id=1, source_target_pairs={{0,32},{32,0},{1,33},{33,1},{2,34},{34,2},{3,35},{35,3},{4,36},{36... | collective-permute-start | bytes 589832 | tf_op jit(solution)/shard_map/ppermute | solution.py:257
  8.6 9.4 %collective-permute-start.4 = (f16[400,128]{1,0:T(8,128)(2,1)S(1)}, f16[400,128]{1,0:T(8,128)(2,1)S(1)}, u32[]{:S(2)}, u32[]{:S(2)}) collective-permute-start(f16[400,128]{1,0:T(8,128)(2,1)S(1)} %get-tuple-element.47), channel_id=1, source_target_pairs={{0,128},{64,192},{128,0},{192,64},{1,129},{65,193},{129,1},{193,65... | collective-permute-start | bytes 307208 | tf_op jit(solution)/shard_map/ppermute | solution.py:261
  14.0 6.9 %collective-permute-start.3 = (f16[400,128]{1,0:T(8,128)(2,1)S(1)}, f16[400,128]{1,0:T(8,128)(2,1)S(1)}, u32[]{:S(2)}, u32[]{:S(2)}) collective-permute-start(f16[400,128]{1,0:T(8,128)(2,1)S(1)} %convert_element_type.22), channel_id=1, source_target_pairs={{0,64},{64,128},{128,192},{192,0},{1,65},{65,129},{129,193},{193,1... | collective-permute-start | bytes 307208 | tf_op jit(solution)/shard_map/ppermute | solution.py:261
  15.3 9.0 %collective-permute-start.5 = (f16[400,128]{1,0:T(8,128)(2,1)S(1)}, f16[400,128]{1,0:T(8,128)(2,1)S(1)}, u32[]{:S(2)}, u32[]{:S(2)}) collective-permute-start(f16[400,128]{1,0:T(8,128)(2,1)S(1)} %convert_element_type.26), channel_id=1, source_target_pairs={{0,192},{64,0},{128,64},{192,128},{1,193},{65,1},{129,65},{193,129... | collective-permute-start | bytes 307208 | tf_op jit(solution)/shard_map/ppermute | solution.py:261

commit v3 on v2

--- a/solution.py
+++ b/solution.py
@@ -59,11 +59,11 @@
         for t, weight in enumerate(weights):
             source = weight.at[:, pl.ds(first, 2)]
             copies.append(pltpu.make_async_copy(source, held.at[i, t], done.at[i, t]))
-    for copy in copies:
-        copy.start()
     if steps == STEPS[:1]:
         gate_copy = pltpu.make_async_copy(gate, gate_held, gate_done)
         gate_copy.start()
+    for copy in copies:
+        copy.start()
     for i in range(len(steps)):
         for t in range(3):
             copies[3 * i + t].wait()
@@ -148,11 +148,11 @@
         for r in range(2):
             for t in range(3):
                 for e in range(2):
-                    total = put(total, whole(part[r, t, e]), (row == r * 4 + t) & (lane == expert + e))
+                    total = put(total, whole(part[r, t, e]), (row == t) & (lane == r * 8 + expert + e))
     for r in range(2):
         gate_rows = jnp.sum(gate_parts[r], axis=1, keepdims=True)
         for e in range(8):
-            total = put(total, gate_rows[e : e + 1, :], (row == r * 4 + 3) & (lane == e))
+            total = put(total, gate_rows[e : e + 1, :], (row == 3) & (lane == r * 8 + e))
     small[...] = total
 
 
@@ -171,24 +171,26 @@
     serve_gate = (((gates[0] + gates[1]) + (gates[2] + gates[3])) * factor).astype(jnp.bfloat16)
     gate = serve_gate.astype(F32)
 
-    lane = lax.broadcasted_iota(jnp.int32, (8, width), 1)
-    row = lax.broadcasted_iota(jnp.int32, (8, width), 0)
+    lane = lax.broadcasted_iota(jnp.int32, (4, width), 1)
+    row = lax.broadcasted_iota(jnp.int32, (4, width), 0)
     small = counted[...]
     for t in range(3):
         total = jnp.sum(fold(held[t * hidden : (t + 1) * hidden, :]), axis=0, keepdims=True)
-        total = jnp.broadcast_to(jnp.sum(total, axis=1, keepdims=True), (8, width))
-        small = jnp.where((row == 0) & (lane == 16 + t), total, small)
-    squares = jnp.broadcast_to(jnp.sum(gate * gate, axis=1, keepdims=True), (8, width))
-    small = jnp.where((row == line * 2 + core) & (lane == 19), squares, small)
+        total = jnp.broadcast_to(jnp.sum(total, axis=1, keepdims=True), (4, width))
+        small = jnp.where((row == t) & (lane == 16), total, small)
+    own_row = lax.broadcasted_iota(jnp.int32, gate.shape, 0) == line * 2 + core
+    squares = jnp.sum(jnp.where(own_row, gate * gate, 0.0), axis=0, keepdims=True)
+    squares = jnp.broadcast_to(jnp.sum(squares, axis=1, keepdims=True), (4, width))
+    small = jnp.where((row == 3) & (lane == 16), squares, small)
     high = small.astype(jnp.bfloat16).astype(F32)
     small = (high + pltpu.roll(small - high, width // 2, 1)).astype(jnp.bfloat16)
     for peer in range(peers):
         out[peer, :8, :] = serve_gate
-        out[peer, 8:16, :] = small
         for t in range(3):
-            start = 16 + t * each
+            start = 8 + t * each
             source = t * hidden + peer * each
             out[peer, start : start + each, :] = held[source : source + each, :].astype(jnp.bfloat16)
+        out[peer, 8 + 3 * each :, :] = small
 
 
 def finish(arrived, out1, out3, out2, gate, soup, replica):
@@ -199,19 +201,19 @@
         columns = pl.ds(peer * width, width)
         gate[:, columns] = arrived[peer, :experts, :]
         for k, out in enumerate((out1, out3, out2)):
-            start = 2 * experts + k * each
+            start = experts + k * each
             out[0, :, columns] = arrived[peer, start : start + each, :]
-    sums = jnp.sum(arrived[:, experts : 2 * experts, :].astype(F32), axis=0)
+    sums = jnp.sum(arrived[:, experts + 3 * each :, :].astype(F32), axis=0)
     sums = sums + pltpu.roll(sums, width // 2, 1)
-    over_rows = jnp.sum(sums, axis=0, keepdims=True)
     lane = lax.broadcasted_iota(jnp.int32, sums.shape, 1)
-    column = jnp.where(lane < 2 * experts, lax.broadcasted_iota(jnp.int32, sums.shape, 0), lane)
+    row = lax.broadcasted_iota(jnp.int32, sums.shape, 0)
     row_entries = peers * width
-    entries = jnp.where(lax.rem(column, 4) == 3, row_entries, peers * each * row_entries)
-    sums = jnp.where(lane < 2 * experts, sums, over_rows)
+    entries = jnp.where(row == 3, row_entries, peers * each * row_entries)
     norms = jnp.sqrt(sums / entries.astype(F32))
-    replica[...] = norms[:, :experts]
-    soup[...] = pltpu.roll(norms, width - 2 * experts, 1)[:1, :4]
+    replica[:4, :] = norms[:, :experts]
+    replica[4:, :] = pltpu.roll(norms, width - experts, 1)[:, :experts]
+    column = jnp.sum(jnp.where(lane == 2 * experts, norms, 0.0), axis=1, keepdims=True)
+    soup[...] = jnp.sum(jnp.where(lane == row, column, 0.0), axis=0, keepdims=True)[:, :4]
 
 
 def steps(rep_w1, rep_w3, rep_w2, rep_gate):
@@ -268,12 +270,12 @@
     )
     came[STEPS[1]] = along(plus, STEPS[1])
     came[STEPS[2]] = along(minus, STEPS[2])
-    counted = call(functools.partial(count, lines), array((8, width)), 1 << 20)(
+    counted = call(functools.partial(count, lines), array((4, width)), 1 << 20)(
         far_parts, near_parts, own_parts, gate_parts
     )
     message = call(
         functools.partial(combine, peers, lines),
-        array((peers, 32, width), jnp.bfloat16),
+        array((peers, experts + 3 * each + 4, width), jnp.bfloat16),
         1 << 22,
         (pltpu.VMEM((rows, width), F32),),
     )(own_kept, own_came, came[1], came[2], came[3], far.astype(jnp.float16).astype(F32), counted)

time: 40.6 us -> 40.4 us (level)
  no operation moved by 1% of the time
where the time goes in v3:
time: 40.4 us; the launch traced here: 40.2 us
  blocking collectives  14.8 us (37%)
  starting transfers between devices  13 us (32%)
  waiting for transfers between devices  6.37 us (16%)
  Pallas kernels  5.28 us (13%)
  between operations  0.74 us (2%)
    all_to_all x1, blocking collectives, steps(): arrived = lax.all_to_all(message, SA, 0, 0, tiled=True)  14.8 us
    ppermute x3, starting transfers between devices, along(): return lax.ppermute(message.astype(jnp.float16), 'zh', pairs).astype(F32)  9.02 us
    ppermute x3, waiting for transfers between devices, along(): return lax.ppermute(message.astype(jnp.float16), 'zh', pairs).astype(F32)  6.36 us
    pallas_call x8, Pallas kernels, run(): pl.pallas_call(kernel, out_shape=out_shape, in_specs=specs, out_specs=jax...  5.28 us
    ppermute x1, starting transfers between devices, steps(): far_came = lax.ppermute(far_sent, 'c', swap)  3.29 us
  transfers between devices with their start and end apart: 6, of which 2 were waited for; matrix products, arithmetic and copies ran while one was open for 0% of the time, Pallas kernels for 7%

profile of v3, /device:TPU:1, one launch (start us, length us, event | category | flops | bytes accessed | tf_op | source)
XLA Modules:
  0.0 40.2 jit_solution(11981265328119221372)
XLA Ops:
  0.6 1.2 %shard_map.91 = (f32[392,128]{1,0:T(8,128)S(1)}, f32[384,128]{1,0:T(8,128)S(1)}, f32[1,2,3,2,8,128]{5,4,3,2,1,0:T(8,128)S(1)}, f32[2,8,128]{2,1,0:T(8,128)S(1)}) custom-call(f32[2,8,128,128]{3,2,1,0:T(8,128)} %refs_0_.5, f32[2,8,128,128]{3,2,1,0:T(8,128)} %refs_1_.5, f32[2,8,128,128]{3,2,1,0:T(8,128)} %refs_2_.5, f32[2,8,128]{2,1,0:T(8,128)} %refs_3_.1), custom_call_target="tpu_custom_call" | custom-call | flops 4194304 | tf_op jit(solution)/shard_map/pallas_call | solution.py:26
  1.8 3.3 %collective-permute-start.2 = (f32[392,128]{1,0:T(8,128)S(1)}, f32[392,128]{1,0:T(8,128)S(1)}, u32[]{:S(2)}, u32[]{:S(2)}) collective-permute-start(f32[392,128]{1,0:T(8,128)S(1)} %get-tuple-element.32.sent), channel_id=1, source_target_pairs={{0,32},{32,0},{1,33},{33,1},{2,34},{34,2},{3,35},{35,3},{4,36},{36... | collective-permute-start | bytes 602120 | tf_op jit(solution)/shard_map/ppermute | solution.py:243
  5.1 1.4 %shard_map.93 = (f32[768,128]{1,0:T(8,128)S(1)}, f32[768,128]{1,0:T(8,128)S(1)}, f32[2,2,3,2,8,128]{5,4,3,2,1,0:T(8,128)S(1)}) custom-call(f32[2,8,128,128]{3,2,1,0:T(8,128)} %refs_0_.5, f32[2,8,128,128]{3,2,1,0:T(8,128)} %refs_1_.5, f32[2,8,128,128]{3,2,1,0:T(8,128)} %refs_2_.5, f32[2,8,128]{2,1,0:T(8,128)S(1)} %get-tuple-element.26.refs_3_.gate_parts), custom_call_target="tpu_custom_call" | custom-call | flops 8388608 | tf_op jit(solution)/shard_map/pallas_call | solution.py:26
  6.6 0.1 collective-permute-start.1
  6.7 1.2 %shard_map.92 = (f32[384,128]{1,0:T(8,128)S(1)}, f32[384,128]{1,0:T(8,128)S(1)}, f32[1,2,3,2,8,128]{5,4,3,2,1,0:T(8,128)S(1)}) custom-call(f32[2,8,128,128]{3,2,1,0:T(8,128)} %refs_0_.5, f32[2,8,128,128]{3,2,1,0:T(8,128)} %refs_1_.5, f32[2,8,128,128]{3,2,1,0:T(8,128)} %refs_2_.5, f32[2,8,128]{2,1,0:T(8,128)S(1)} %get-tuple-element.26.refs_3_.gate_parts), custom_call_target="tpu_custom_call" | custom-call | flops 4194304 | tf_op jit(solution)/shard_map/pallas_call | solution.py:26
  7.9 0.6 %collective-permute-start = (f32[384,128]{1,0:T(8,128)S(1)}, f32[384,128]{1,0:T(8,128)S(1)}, u32[]{:S(2)}, u32[]{:S(2)}) collective-permute-start(f32[384,128]{1,0:T(8,128)S(1)} %get-tuple-element.28), channel_id=1, source_target_pairs={{0,32},{32,0},{1,33},{33,1},{2,34},{34,2},{3,35},{35,3},{4,36},{36... | collective-permute-start | bytes 589832 | tf_op jit(solution)/shard_map/ppermute | solution.py:259
  8.4 0.0 collective-permute-done.2.came
  8.4 0.1 shard_map.94
  8.6 5.3 %collective-permute-start.4 = (f16[400,128]{1,0:T(8,128)(2,1)S(1)}, f16[400,128]{1,0:T(8,128)(2,1)S(1)}, u32[]{:S(2)}, u32[]{:S(2)}) collective-permute-start(f16[400,128]{1,0:T(8,128)(2,1)S(1)} %get-tuple-element.47), channel_id=1, source_target_pairs={{0,128},{64,192},{128,0},{192,64},{1,129},{65,193},{129,1},{193,65... | collective-permute-start | bytes 307208 | tf_op jit(solution)/shard_map/ppermute | solution.py:263
  13.8 0.0 collective-permute-done.1.came
  13.8 0.1 shard_map.95
  14.0 1.3 %collective-permute-start.3 = (f16[400,128]{1,0:T(8,128)(2,1)S(1)}, f16[400,128]{1,0:T(8,128)(2,1)S(1)}, u32[]{:S(2)}, u32[]{:S(2)}) collective-permute-start(f16[400,128]{1,0:T(8,128)(2,1)S(1)} %convert_element_type.22), channel_id=1, source_target_pairs={{0,64},{64,128},{128,192},{192,0},{1,65},{65,129},{129,193},{193,1... | collective-permute-start | bytes 307208 | tf_op jit(solution)/shard_map/ppermute | solution.py:263
  15.3 2.5 %collective-permute-start.5 = (f16[400,128]{1,0:T(8,128)(2,1)S(1)}, f16[400,128]{1,0:T(8,128)(2,1)S(1)}, u32[]{:S(2)}, u32[]{:S(2)}) collective-permute-start(f16[400,128]{1,0:T(8,128)(2,1)S(1)} %convert_element_type.26), channel_id=1, source_target_pairs={{0,192},{64,0},{128,64},{192,128},{1,193},{65,1},{129,65},{193,129... | collective-permute-start | bytes 307208 | tf_op jit(solution)/shard_map/ppermute | solution.py:263
  17.7 0.1 shard_map.96.counted
  17.9 0.0 collective-permute-done.4
  17.9 3.0 %collective-permute-done.3 = f16[400,128]{1,0:T(8,128)(2,1)S(1)} collective-permute-done((f16[400,128]{1,0:T(8,128)(2,1)S(1)}, f16[400,128]{1,0:T(8,128)(2,1)S(1)}, u32[]{:S(2)}, u32[]{:S(2)}) %collective-permute-start.3) | collective-permute-done | bytes 102432 | tf_op jit(solution)/shard_map/ppermute | solution.py:263
  20.9 3.4 %collective-permute-done.5 = f16[400,128]{1,0:T(8,128)(2,1)S(1)} collective-permute-done((f16[400,128]{1,0:T(8,128)(2,1)S(1)}, f16[400,128]{1,0:T(8,128)(2,1)S(1)}, u32[]{:S(2)}, u32[]{:S(2)}) %collective-permute-start.5) | collective-permute-done | bytes 102432 | tf_op jit(solution)/shard_map/ppermute | solution.py:263
  24.3 0.0 collective-permute-done.other
  24.3 0.4 shard_map.97
  24.7 14.8 %all_to_all.5.arrived = bf16[32,24,128]{2,1,0:T(8,128)(2,1)S(1)} all-to-all(bf16[32,24,128]{2,1,0:T(8,128)(2,1)S(1)} %shard_map.97), channel_id=1, replica_groups=mesh['zh'=4,'c'=2,'zl'=2,'x'=4,'y'=4] {'zl','x','y'}, dimensions={0} | all-to-all | bytes 393216 | tf_op jit(solution)/shard_map/all_to_all | solution.py:282
  39.5 0.8 %shard_map.98 = (bf16[1,4,4096]{2,1,0:T(4,128)(2,1)}, bf16[1,4,4096]{2,1,0:T(4,128)(2,1)}, bf16[1,4,4096]{2,1,0:T(4,128)(2,1)}, bf16[8,4096]{1,0:T(8,128)(2,1)}, f32[1,4]{1,0:T(1,128)}, /*index=5*/f32[8,8]{1,0:T(8,128)}) custom-call(bf16[32,24,128]{2,1,0:T(8,128)(2,1)S(1)} %all_to_all.5.arrived), custom_call_target="tpu_custom_call" | custom-call | flops 1048576 | tf_op jit(solution)/shard_map/pallas_call | solution.py:26
  (6 shorter events, 0.1 us)
Async XLA Ops:
  1.8 6.6 %collective-permute-start.2 = (f32[392,128]{1,0:T(8,128)S(1)}, f32[392,128]{1,0:T(8,128)S(1)}, u32[]{:S(2)}, u32[]{:S(2)}) collective-permute-start(f32[392,128]{1,0:T(8,128)S(1)} %get-tuple-element.32.sent), channel_id=1, source_target_pairs={{0,32},{32,0},{1,33},{33,1},{2,34},{34,2},{3,35},{35,3},{4,36},{36... | collective-permute-start | bytes 602120 | tf_op jit(solution)/shard_map/ppermute | solution.py:243
  6.6 7.3 %collective-permute-start.1 = (f32[768,128]{1,0:T(8,128)S(1)}, f32[768,128]{1,0:T(8,128)S(1)}, u32[]{:S(2)}, u32[]{:S(2)}) collective-permute-start(f32[768,128]{1,0:T(8,128)S(1)} %get-tuple-element.30), channel_id=1, source_target_pairs={{0,32},{32,0},{1,33},{33,1},{2,34},{34,2},{3,35},{35,3},{4,36},{36... | collective-permute-start | bytes 1179656 | tf_op jit(solution)/shard_map/ppermute | solution.py:251
  7.9 16.5 %collective-permute-start = (f32[384,128]{1,0:T(8,128)S(1)}, f32[384,128]{1,0:T(8,128)S(1)}, u32[]{:S(2)}, u32[]{:S(2)}) collective-permute-start(f32[384,128]{1,0:T(8,128)S(1)} %get-tuple-element.28), channel_id=1, source_target_pairs={{0,32},{32,0},{1,33},{33,1},{2,34},{34,2},{3,35},{35,3},{4,36},{36... | collective-permute-start | bytes 589832 | tf_op jit(solution)/shard_map/ppermute | solution.py:259
  8.6 9.4 %collective-permute-start.4 = (f16[400,128]{1,0:T(8,128)(2,1)S(1)}, f16[400,128]{1,0:T(8,128)(2,1)S(1)}, u32[]{:S(2)}, u32[]{:S(2)}) collective-permute-start(f16[400,128]{1,0:T(8,128)(2,1)S(1)} %get-tuple-element.47), channel_id=1, source_target_pairs={{0,128},{64,192},{128,0},{192,64},{1,129},{65,193},{129,1},{193,65... | collective-permute-start | bytes 307208 | tf_op jit(solution)/shard_map/ppermute | solution.py:263
  14.0 6.9 %collective-permute-start.3 = (f16[400,128]{1,0:T(8,128)(2,1)S(1)}, f16[400,128]{1,0:T(8,128)(2,1)S(1)}, u32[]{:S(2)}, u32[]{:S(2)}) collective-permute-start(f16[400,128]{1,0:T(8,128)(2,1)S(1)} %convert_element_type.22), channel_id=1, source_target_pairs={{0,64},{64,128},{128,192},{192,0},{1,65},{65,129},{129,193},{193,1... | collective-permute-start | bytes 307208 | tf_op jit(solution)/shard_map/ppermute | solution.py:263
  15.3 9.0 %collective-permute-start.5 = (f16[400,128]{1,0:T(8,128)(2,1)S(1)}, f16[400,128]{1,0:T(8,128)(2,1)S(1)}, u32[]{:S(2)}, u32[]{:S(2)}) collective-permute-start(f16[400,128]{1,0:T(8,128)(2,1)S(1)} %convert_element_type.26), channel_id=1, source_target_pairs={{0,192},{64,0},{128,64},{192,128},{1,193},{65,1},{129,65},{193,129... | collective-permute-start | bytes 307208 | tf_op jit(solution)/shard_map/ppermute | solution.py:263

commit v4 on v3

--- a/solution.py
+++ b/solution.py
@@ -10,7 +10,8 @@
 
 
 ROW = ("zh", "c")
-SA = ("zl", "x", "y")
+SA = "sa"
+FIRST = 26
 FULL = 32768.0
 LEAST = 2.0**-100
 TINY = 2.0**-30
@@ -188,7 +189,7 @@
         out[peer, :8, :] = serve_gate
         for t in range(3):
             start = 8 + t * each
-            source = t * hidden + peer * each
+            source = t * hidden + (peer ^ FIRST) * each
             out[peer, start : start + each, :] = held[source : source + each, :].astype(jnp.bfloat16)
         out[peer, 8 + 3 * each :, :] = small
 
@@ -198,7 +199,7 @@
     experts = gate.shape[0]
     each = out1.shape[1]
     for peer in range(peers):
-        columns = pl.ds(peer * width, width)
+        columns = pl.ds((peer ^ FIRST) * width, width)
         gate[:, columns] = arrived[peer, :experts, :]
         for k, out in enumerate((out1, out3, out2)):
             start = experts + k * each
@@ -279,7 +280,9 @@
         1 << 22,
         (pltpu.VMEM((rows, width), F32),),
     )(own_kept, own_came, came[1], came[2], came[3], far.astype(jnp.float16).astype(F32), counted)
-    arrived = lax.all_to_all(message, SA, 0, 0, tiled=True)
+    arrived = lax.all_to_all(
+        message, SA, 0, 0, axis_index_groups=[[peer ^ FIRST for peer in range(peers)]], tiled=True
+    )
     shard = array((1, each, model_width), jnp.bfloat16)
     *served, soup_norms, replica_norms = call(
         finish,
@@ -298,7 +301,7 @@
 
 
 def solution(mesh):
-    torus = Mesh(mesh.devices.reshape(mesh.shape["row"] // 2, 2, 2, 4, 4), ROW + SA)
+    torus = Mesh(mesh.devices.reshape(mesh.shape["row"] // 2, 2, -1), (*ROW, SA))
     in_specs = (
         P(ROW, None, None, SA),
         P(ROW, None, None, SA),

time: 40.4 us -> 37.6 us (0.931)
  blocking collectives: 14.8 us -> 11.8 us
    all_to_all x1, blocking collectives: 14.8 us -> 11.8 us  [steps(): lax.all_to_all(message, SA, 0, 0, axis_index_groups=[[peer ^ FIRST for pe...]
  transfers between devices with their start and end apart: 6 -> 6, of which waited for: 2 -> 2; matrix products, arithmetic and copies ran while one was open for 0% -> 0% of each run, Pallas kernels for 7% -> 8%
where the time goes in v4:
time: 37.6 us; the launch traced here: 37.3 us
  starting transfers between devices  13 us (35%)
  blocking collectives  11.8 us (31%)
  waiting for transfers between devices  6.37 us (17%)
  Pallas kernels  5.28 us (14%)
  between operations  0.74 us (2%)
    all_to_all x1, blocking collectives, steps(): lax.all_to_all(message, SA, 0, 0, axis_index_groups=[[peer ^ FIRST for pe...  11.8 us
    ppermute x3, starting transfers between devices, along(): return lax.ppermute(message.astype(jnp.float16), 'zh', pairs).astype(F32)  9.02 us
    ppermute x3, waiting for transfers between devices, along(): return lax.ppermute(message.astype(jnp.float16), 'zh', pairs).astype(F32)  6.36 us
    pallas_call x8, Pallas kernels, run(): pl.pallas_call(kernel, out_shape=out_shape, in_specs=specs, out_specs=jax...  5.28 us
    ppermute x1, starting transfers between devices, steps(): far_came = lax.ppermute(far_sent, 'c', swap)  3.29 us
  transfers between devices with their start and end apart: 6, of which 2 were waited for; matrix products, arithmetic and copies ran while one was open for 0% of the time, Pallas kernels for 8%

profile of v4, /device:TPU:1, one launch (start us, length us, event | category | flops | bytes accessed | tf_op | source)
XLA Modules:
  0.0 37.3 jit_solution(13041506588002279018)
XLA Ops:
  0.6 1.2 %shard_map.91 = (f32[392,128]{1,0:T(8,128)S(1)}, f32[384,128]{1,0:T(8,128)S(1)}, f32[1,2,3,2,8,128]{5,4,3,2,1,0:T(8,128)S(1)}, f32[2,8,128]{2,1,0:T(8,128)S(1)}) custom-call(f32[2,8,128,128]{3,2,1,0:T(8,128)} %refs_0_.5, f32[2,8,128,128]{3,2,1,0:T(8,128)} %refs_1_.5, f32[2,8,128,128]{3,2,1,0:T(8,128)} %refs_2_.5, f32[2,8,128]{2,1,0:T(8,128)} %refs_3_.1), custom_call_target="tpu_custom_call" | custom-call | flops 4194304 | tf_op jit(solution)/shard_map/pallas_call | solution.py:27
  1.8 3.3 %collective-permute-start.2 = (f32[392,128]{1,0:T(8,128)S(1)}, f32[392,128]{1,0:T(8,128)S(1)}, u32[]{:S(2)}, u32[]{:S(2)}) collective-permute-start(f32[392,128]{1,0:T(8,128)S(1)} %get-tuple-element.32.sent), channel_id=1, source_target_pairs={{0,32},{32,0},{1,33},{33,1},{2,34},{34,2},{3,35},{35,3},{4,36},{36... | collective-permute-start | bytes 602120 | tf_op jit(solution)/shard_map/ppermute | solution.py:244
  5.1 1.4 %shard_map.93 = (f32[768,128]{1,0:T(8,128)S(1)}, f32[768,128]{1,0:T(8,128)S(1)}, f32[2,2,3,2,8,128]{5,4,3,2,1,0:T(8,128)S(1)}) custom-call(f32[2,8,128,128]{3,2,1,0:T(8,128)} %refs_0_.5, f32[2,8,128,128]{3,2,1,0:T(8,128)} %refs_1_.5, f32[2,8,128,128]{3,2,1,0:T(8,128)} %refs_2_.5, f32[2,8,128]{2,1,0:T(8,128)S(1)} %get-tuple-element.26.refs_3_.gate_parts), custom_call_target="tpu_custom_call" | custom-call | flops 8388608 | tf_op jit(solution)/shard_map/pallas_call | solution.py:27
  6.6 0.1 collective-permute-start.1
  6.7 1.2 %shard_map.92 = (f32[384,128]{1,0:T(8,128)S(1)}, f32[384,128]{1,0:T(8,128)S(1)}, f32[1,2,3,2,8,128]{5,4,3,2,1,0:T(8,128)S(1)}) custom-call(f32[2,8,128,128]{3,2,1,0:T(8,128)} %refs_0_.5, f32[2,8,128,128]{3,2,1,0:T(8,128)} %refs_1_.5, f32[2,8,128,128]{3,2,1,0:T(8,128)} %refs_2_.5, f32[2,8,128]{2,1,0:T(8,128)S(1)} %get-tuple-element.26.refs_3_.gate_parts), custom_call_target="tpu_custom_call" | custom-call | flops 4194304 | tf_op jit(solution)/shard_map/pallas_call | solution.py:27
  7.9 0.6 %collective-permute-start = (f32[384,128]{1,0:T(8,128)S(1)}, f32[384,128]{1,0:T(8,128)S(1)}, u32[]{:S(2)}, u32[]{:S(2)}) collective-permute-start(f32[384,128]{1,0:T(8,128)S(1)} %get-tuple-element.28), channel_id=1, source_target_pairs={{0,32},{32,0},{1,33},{33,1},{2,34},{34,2},{3,35},{35,3},{4,36},{36... | collective-permute-start | bytes 589832 | tf_op jit(solution)/shard_map/ppermute | solution.py:260
  8.4 0.0 collective-permute-done.2.came
  8.4 0.1 shard_map.94
  8.6 5.3 %collective-permute-start.4 = (f16[400,128]{1,0:T(8,128)(2,1)S(1)}, f16[400,128]{1,0:T(8,128)(2,1)S(1)}, u32[]{:S(2)}, u32[]{:S(2)}) collective-permute-start(f16[400,128]{1,0:T(8,128)(2,1)S(1)} %get-tuple-element.47), channel_id=1, source_target_pairs={{0,128},{64,192},{128,0},{192,64},{1,129},{65,193},{129,1},{193,65... | collective-permute-start | bytes 307208 | tf_op jit(solution)/shard_map/ppermute | solution.py:264
  13.8 0.0 collective-permute-done.1.came
  13.8 0.1 shard_map.95
  14.0 1.3 %collective-permute-start.3 = (f16[400,128]{1,0:T(8,128)(2,1)S(1)}, f16[400,128]{1,0:T(8,128)(2,1)S(1)}, u32[]{:S(2)}, u32[]{:S(2)}) collective-permute-start(f16[400,128]{1,0:T(8,128)(2,1)S(1)} %convert_element_type.22), channel_id=1, source_target_pairs={{0,64},{64,128},{128,192},{192,0},{1,65},{65,129},{129,193},{193,1... | collective-permute-start | bytes 307208 | tf_op jit(solution)/shard_map/ppermute | solution.py:264
  15.3 2.5 %collective-permute-start.5 = (f16[400,128]{1,0:T(8,128)(2,1)S(1)}, f16[400,128]{1,0:T(8,128)(2,1)S(1)}, u32[]{:S(2)}, u32[]{:S(2)}) collective-permute-start(f16[400,128]{1,0:T(8,128)(2,1)S(1)} %convert_element_type.26), channel_id=1, source_target_pairs={{0,192},{64,0},{128,64},{192,128},{1,193},{65,1},{129,65},{193,129... | collective-permute-start | bytes 307208 | tf_op jit(solution)/shard_map/ppermute | solution.py:264
  17.7 0.1 shard_map.96.counted
  17.9 0.0 collective-permute-done.4
  17.9 3.0 %collective-permute-done.3 = f16[400,128]{1,0:T(8,128)(2,1)S(1)} collective-permute-done((f16[400,128]{1,0:T(8,128)(2,1)S(1)}, f16[400,128]{1,0:T(8,128)(2,1)S(1)}, u32[]{:S(2)}, u32[]{:S(2)}) %collective-permute-start.3) | collective-permute-done | bytes 102432 | tf_op jit(solution)/shard_map/ppermute | solution.py:264
  20.9 3.4 %collective-permute-done.5 = f16[400,128]{1,0:T(8,128)(2,1)S(1)} collective-permute-done((f16[400,128]{1,0:T(8,128)(2,1)S(1)}, f16[400,128]{1,0:T(8,128)(2,1)S(1)}, u32[]{:S(2)}, u32[]{:S(2)}) %collective-permute-start.5) | collective-permute-done | bytes 102432 | tf_op jit(solution)/shard_map/ppermute | solution.py:264
  24.3 0.0 collective-permute-done.other
  24.3 0.4 shard_map.97
  24.7 11.8 %all_to_all.5.arrived = bf16[32,24,128]{2,1,0:T(8,128)(2,1)S(1)} all-to-all(bf16[32,24,128]{2,1,0:T(8,128)(2,1)S(1)} %shard_map.97), channel_id=1, replica_groups={{26,27,24,25,30,31,28,29,18,19,16,17,22,23,20,21,10,11,8,9,14,15,12,13,..., dimensions={0} | all-to-all | bytes 393216 | tf_op jit(solution)/shard_map/all_to_all | solution.py:283
  36.5 0.8 %shard_map.98 = (bf16[1,4,4096]{2,1,0:T(4,128)(2,1)}, bf16[1,4,4096]{2,1,0:T(4,128)(2,1)}, bf16[1,4,4096]{2,1,0:T(4,128)(2,1)}, bf16[8,4096]{1,0:T(8,128)(2,1)}, f32[1,4]{1,0:T(1,128)}, /*index=5*/f32[8,8]{1,0:T(8,128)}) custom-call(bf16[32,24,128]{2,1,0:T(8,128)(2,1)S(1)} %all_to_all.5.arrived), custom_call_target="tpu_custom_call" | custom-call | flops 1048576 | tf_op jit(solution)/shard_map/pallas_call | solution.py:27
  (6 shorter events, 0.1 us)
Async XLA Ops:
  1.8 6.6 %collective-permute-start.2 = (f32[392,128]{1,0:T(8,128)S(1)}, f32[392,128]{1,0:T(8,128)S(1)}, u32[]{:S(2)}, u32[]{:S(2)}) collective-permute-start(f32[392,128]{1,0:T(8,128)S(1)} %get-tuple-element.32.sent), channel_id=1, source_target_pairs={{0,32},{32,0},{1,33},{33,1},{2,34},{34,2},{3,35},{35,3},{4,36},{36... | collective-permute-start | bytes 602120 | tf_op jit(solution)/shard_map/ppermute | solution.py:244
  6.6 7.3 %collective-permute-start.1 = (f32[768,128]{1,0:T(8,128)S(1)}, f32[768,128]{1,0:T(8,128)S(1)}, u32[]{:S(2)}, u32[]{:S(2)}) collective-permute-start(f32[768,128]{1,0:T(8,128)S(1)} %get-tuple-element.30), channel_id=1, source_target_pairs={{0,32},{32,0},{1,33},{33,1},{2,34},{34,2},{3,35},{35,3},{4,36},{36... | collective-permute-start | bytes 1179656 | tf_op jit(solution)/shard_map/ppermute | solution.py:252
  7.9 16.5 %collective-permute-start = (f32[384,128]{1,0:T(8,128)S(1)}, f32[384,128]{1,0:T(8,128)S(1)}, u32[]{:S(2)}, u32[]{:S(2)}) collective-permute-start(f32[384,128]{1,0:T(8,128)S(1)} %get-tuple-element.28), channel_id=1, source_target_pairs={{0,32},{32,0},{1,33},{33,1},{2,34},{34,2},{3,35},{35,3},{4,36},{36... | collective-permute-start | bytes 589832 | tf_op jit(solution)/shard_map/ppermute | solution.py:260
  8.6 9.4 %collective-permute-start.4 = (f16[400,128]{1,0:T(8,128)(2,1)S(1)}, f16[400,128]{1,0:T(8,128)(2,1)S(1)}, u32[]{:S(2)}, u32[]{:S(2)}) collective-permute-start(f16[400,128]{1,0:T(8,128)(2,1)S(1)} %get-tuple-element.47), channel_id=1, source_target_pairs={{0,128},{64,192},{128,0},{192,64},{1,129},{65,193},{129,1},{193,65... | collective-permute-start | bytes 307208 | tf_op jit(solution)/shard_map/ppermute | solution.py:264
  14.0 6.9 %collective-permute-start.3 = (f16[400,128]{1,0:T(8,128)(2,1)S(1)}, f16[400,128]{1,0:T(8,128)(2,1)S(1)}, u32[]{:S(2)}, u32[]{:S(2)}) collective-permute-start(f16[400,128]{1,0:T(8,128)(2,1)S(1)} %convert_element_type.22), channel_id=1, source_target_pairs={{0,64},{64,128},{128,192},{192,0},{1,65},{65,129},{129,193},{193,1... | collective-permute-start | bytes 307208 | tf_op jit(solution)/shard_map/ppermute | solution.py:264
  15.3 9.0 %collective-permute-start.5 = (f16[400,128]{1,0:T(8,128)(2,1)S(1)}, f16[400,128]{1,0:T(8,128)(2,1)S(1)}, u32[]{:S(2)}, u32[]{:S(2)}) collective-permute-start(f16[400,128]{1,0:T(8,128)(2,1)S(1)} %convert_element_type.26), channel_id=1, source_target_pairs={{0,192},{64,0},{128,64},{192,128},{1,193},{65,1},{129,65},{193,129... | collective-permute-start | bytes 307208 | tf_op jit(solution)/shard_map/ppermute | solution.py:264

commit v5 on v4

--- a/solution.py
+++ b/solution.py
@@ -15,7 +15,14 @@
 FULL = 32768.0
 LEAST = 2.0**-100
 TINY = 2.0**-30
-STEPS = (2, 1, 3)
+STEPS = (1, 2, 3)
+TO = ((0, 1, 2, 3), (3, 2, 0, 1), (1, 0, 3, 2), (2, 3, 1, 0))
+
+
+def partner(line, step):
+    return sum(jnp.where(line == k, to, 0) for k, to in enumerate(TO[step]))
+
+
 ROOM = 6 << 20
 F32 = jnp.float32
 
@@ -46,7 +53,7 @@
     return jnp.sum((values * values).reshape(rows // 8, 8, width), axis=0)
 
 
-def local(steps, lines, *refs):
+def local(steps, *refs):
     weights, refs = refs[:3], refs[3:]
     if steps == STEPS[:1]:
         gate, sent, kept, parts, gate_parts, held, gate_held, done, gate_done = refs
@@ -56,7 +63,7 @@
     hidden = held.shape[-2]
     copies = []
     for i, step in enumerate(steps):
-        first = 2 * lax.rem(line + step, lines)
+        first = 2 * partner(line, step)
         for t, weight in enumerate(weights):
             source = weight.at[:, pl.ds(first, 2)]
             copies.append(pltpu.make_async_copy(source, held.at[i, t], done.at[i, t]))
@@ -130,7 +137,7 @@
         write(message, blocks + [far[...]])
 
 
-def count(lines, far_parts, near_parts, own_parts, gate_parts, small):
+def count(far_parts, near_parts, own_parts, gate_parts, small):
     line = lax.axis_index("zh")
     shape = small.shape
     lane = lax.broadcasted_iota(jnp.int32, shape, 1)
@@ -145,7 +152,7 @@
 
     for i, step in enumerate((*STEPS, 0)):
         part = (far_parts.at[0], near_parts.at[0], near_parts.at[1], own_parts.at[0])[i]
-        expert = 2 * lax.rem(line + step, lines)
+        expert = 2 * partner(line, step)
         for r in range(2):
             for t in range(3):
                 for e in range(2):
@@ -234,7 +241,7 @@
         return (pltpu.VMEM((n, 3, held, 2, hidden, width), F32),)
 
     far_sent, far_kept, far_parts, gate_parts = call(
-        functools.partial(local, STEPS[:1], lines),
+        functools.partial(local, STEPS[:1]),
         (array((rows + 8, width)), array((rows, width)), array((1, held, 3, 2, 8, width)), array((held, 8, width))),
         1 << 22,
         buffers(1)
@@ -243,7 +250,7 @@
     )(*weights, rep_gate)
     far_came = lax.ppermute(far_sent, "c", swap)
     near_sent, near_kept, near_parts = call(
-        functools.partial(local, STEPS[1:], lines),
+        functools.partial(local, STEPS[1:]),
         (array((2 * rows, width)), array((2 * rows, width)), array((2, held, 3, 2, 8, width))),
         1 << 23,
         buffers(2) + (pltpu.SemaphoreType.DMA((2, 3)),),
@@ -251,7 +258,7 @@
     )(*weights, gate_parts)
     near_came = lax.ppermute(near_sent, "c", swap)
     own_sent, own_kept, own_parts = call(
-        functools.partial(local, (0,), lines),
+        functools.partial(local, (0,)),
         (array((rows, width)), array((rows, width)), array((1, held, 3, 2, 8, width))),
         1 << 22,
         buffers(1) + (pltpu.SemaphoreType.DMA((1, 3)),),
@@ -260,7 +267,7 @@
     own_came = lax.ppermute(own_sent, "c", swap)
 
     def along(message, step):
-        pairs = [(i, (i + step) % lines) for i in range(lines)]
+        pairs = list(enumerate(TO[step]))
         return lax.ppermute(message.astype(jnp.float16), "zh", pairs).astype(F32)
 
     half = array((rows + 16, width))
@@ -271,9 +278,7 @@
     )
     came[STEPS[1]] = along(plus, STEPS[1])
     came[STEPS[2]] = along(minus, STEPS[2])
-    counted = call(functools.partial(count, lines), array((4, width)), 1 << 20)(
-        far_parts, near_parts, own_parts, gate_parts
-    )
+    counted = call(count, array((4, width)), 1 << 20)(far_parts, near_parts, own_parts, gate_parts)
     message = call(
         functools.partial(combine, peers, lines),
         array((peers, experts + 3 * each + 4, width), jnp.bfloat16),

time: 37.6 us -> 37.5 us (level)
  waiting for transfers between devices: 6.37 us -> 8.5 us
  starting transfers between devices: 13 us -> 10.9 us
    ppermute x3, waiting for transfers between devices: 6.36 us -> 8.49 us  [along(): return lax.ppermute(message.astype(jnp.float16), 'zh', pairs).astype(F32)]
    ppermute x3, starting transfers between devices: 9.02 us -> 6.9 us  [along(): return lax.ppermute(message.astype(jnp.float16), 'zh', pairs).astype(F32)]
where the time goes in v5:
time: 37.5 us; the launch traced here: 37.3 us
  blocking collectives  11.8 us (31%)
  starting transfers between devices  10.9 us (29%)
  waiting for transfers between devices  8.5 us (23%)
  Pallas kernels  5.27 us (14%)
  between operations  0.74 us (2%)
    all_to_all x1, blocking collectives, steps(): lax.all_to_all(message, SA, 0, 0, axis_index_groups=[[peer ^ FIRST for pe...  11.8 us
    ppermute x3, waiting for transfers between devices, along(): return lax.ppermute(message.astype(jnp.float16), 'zh', pairs).astype(F32)  8.49 us
    ppermute x3, starting transfers between devices, along(): return lax.ppermute(message.astype(jnp.float16), 'zh', pairs).astype(F32)  6.9 us
    pallas_call x8, Pallas kernels, run(): pl.pallas_call(kernel, out_shape=out_shape, in_specs=specs, out_specs=jax...  5.27 us
    ppermute x1, starting transfers between devices, steps(): far_came = lax.ppermute(far_sent, 'c', swap)  3.29 us
  transfers between devices with their start and end apart: 6, of which 2 were waited for; matrix products, arithmetic and copies ran while one was open for 0% of the time, Pallas kernels for 8%

profile of v5, /device:TPU:1, one launch (start us, length us, event | category | flops | bytes accessed | tf_op | source)
XLA Modules:
  0.0 37.3 jit_solution(15700224024478921062)
XLA Ops:
  0.6 1.2 %shard_map.91 = (f32[392,128]{1,0:T(8,128)S(1)}, f32[384,128]{1,0:T(8,128)S(1)}, f32[1,2,3,2,8,128]{5,4,3,2,1,0:T(8,128)S(1)}, f32[2,8,128]{2,1,0:T(8,128)S(1)}) custom-call(f32[2,8,128,128]{3,2,1,0:T(8,128)} %refs_0_.5, f32[2,8,128,128]{3,2,1,0:T(8,128)} %refs_1_.5, f32[2,8,128,128]{3,2,1,0:T(8,128)} %refs_2_.5, f32[2,8,128]{2,1,0:T(8,128)} %refs_3_.1), custom_call_target="tpu_custom_call" | custom-call | flops 4194304 | tf_op jit(solution)/shard_map/pallas_call | solution.py:34
  1.8 3.3 %collective-permute-start.1 = (f32[392,128]{1,0:T(8,128)S(1)}, f32[392,128]{1,0:T(8,128)S(1)}, u32[]{:S(2)}, u32[]{:S(2)}) collective-permute-start(f32[392,128]{1,0:T(8,128)S(1)} %get-tuple-element.30.sent), channel_id=1, source_target_pairs={{0,32},{32,0},{1,33},{33,1},{2,34},{34,2},{3,35},{35,3},{4,36},{36... | collective-permute-start | bytes 602120 | tf_op jit(solution)/shard_map/ppermute | solution.py:251
  5.1 1.4 %shard_map.94 = (f32[768,128]{1,0:T(8,128)S(1)}, f32[768,128]{1,0:T(8,128)S(1)}, f32[2,2,3,2,8,128]{5,4,3,2,1,0:T(8,128)S(1)}) custom-call(f32[2,8,128,128]{3,2,1,0:T(8,128)} %refs_0_.5, f32[2,8,128,128]{3,2,1,0:T(8,128)} %refs_1_.5, f32[2,8,128,128]{3,2,1,0:T(8,128)} %refs_2_.5, f32[2,8,128]{2,1,0:T(8,128)S(1)} %get-tuple-element.26.refs_3_.gate_parts), custom_call_target="tpu_custom_call" | custom-call | flops 8388608 | tf_op jit(solution)/shard_map/pallas_call | solution.py:34
  6.6 0.1 collective-permute-start.3
  6.7 1.2 %shard_map.92 = (f32[384,128]{1,0:T(8,128)S(1)}, f32[384,128]{1,0:T(8,128)S(1)}, f32[1,2,3,2,8,128]{5,4,3,2,1,0:T(8,128)S(1)}) custom-call(f32[2,8,128,128]{3,2,1,0:T(8,128)} %refs_0_.5, f32[2,8,128,128]{3,2,1,0:T(8,128)} %refs_1_.5, f32[2,8,128,128]{3,2,1,0:T(8,128)} %refs_2_.5, f32[2,8,128]{2,1,0:T(8,128)S(1)} %get-tuple-element.26.refs_3_.gate_parts), custom_call_target="tpu_custom_call" | custom-call | flops 4194304 | tf_op jit(solution)/shard_map/pallas_call | solution.py:34
  7.9 0.6 %collective-permute-start = (f32[384,128]{1,0:T(8,128)S(1)}, f32[384,128]{1,0:T(8,128)S(1)}, u32[]{:S(2)}, u32[]{:S(2)}) collective-permute-start(f32[384,128]{1,0:T(8,128)S(1)} %get-tuple-element.28), channel_id=1, source_target_pairs={{0,32},{32,0},{1,33},{33,1},{2,34},{34,2},{3,35},{35,3},{4,36},{36... | collective-permute-start | bytes 589832 | tf_op jit(solution)/shard_map/ppermute | solution.py:267
  8.4 0.0 collective-permute-done.1.came
  8.4 0.1 shard_map.93
  8.6 4.4 %collective-permute-start.2 = (f16[400,128]{1,0:T(8,128)(2,1)S(1)}, f16[400,128]{1,0:T(8,128)(2,1)S(1)}, u32[]{:S(2)}, u32[]{:S(2)}) collective-permute-start(f16[400,128]{1,0:T(8,128)(2,1)S(1)} %get-tuple-element.47), channel_id=1, source_target_pairs={{0,192},{64,128},{128,0},{192,64},{1,193},{65,129},{129,1},{193,65... | collective-permute-start | bytes 307208 | tf_op jit(solution)/shard_map/ppermute | solution.py:271
  12.9 0.0 collective-permute-done.3.came
  12.9 0.1 shard_map.95
  13.1 1.3 %collective-permute-start.4 = (f16[400,128]{1,0:T(8,128)(2,1)S(1)}, f16[400,128]{1,0:T(8,128)(2,1)S(1)}, u32[]{:S(2)}, u32[]{:S(2)}) collective-permute-start(f16[400,128]{1,0:T(8,128)(2,1)S(1)} %convert_element_type.24), channel_id=1, source_target_pairs={{0,64},{64,0},{128,192},{192,128},{1,65},{65,1},{129,193},{193,129... | collective-permute-start | bytes 307208 | tf_op jit(solution)/shard_map/ppermute | solution.py:271
  14.4 1.2 %collective-permute-start.5 = (f16[400,128]{1,0:T(8,128)(2,1)S(1)}, f16[400,128]{1,0:T(8,128)(2,1)S(1)}, u32[]{:S(2)}, u32[]{:S(2)}) collective-permute-start(f16[400,128]{1,0:T(8,128)(2,1)S(1)} %convert_element_type.26), channel_id=1, source_target_pairs={{0,128},{64,192},{128,64},{192,0},{1,129},{65,193},{129,65},{193,1... | collective-permute-start | bytes 307208 | tf_op jit(solution)/shard_map/ppermute | solution.py:271
  15.6 0.1 shard_map.96.counted
  15.8 1.4 %collective-permute-done.2 = f16[400,128]{1,0:T(8,128)(2,1)S(1)} collective-permute-done((f16[400,128]{1,0:T(8,128)(2,1)S(1)}, f16[400,128]{1,0:T(8,128)(2,1)S(1)}, u32[]{:S(2)}, u32[]{:S(2)}) %collective-permute-start.2) | collective-permute-done | bytes 102432 | tf_op jit(solution)/shard_map/ppermute | solution.py:271
  17.2 7.1 %collective-permute-done.4 = f16[400,128]{1,0:T(8,128)(2,1)S(1)} collective-permute-done((f16[400,128]{1,0:T(8,128)(2,1)S(1)}, f16[400,128]{1,0:T(8,128)(2,1)S(1)}, u32[]{:S(2)}, u32[]{:S(2)}) %collective-permute-start.4) | collective-permute-done | bytes 102432 | tf_op jit(solution)/shard_map/ppermute | solution.py:271
  24.3 0.0 collective-permute-done.5
  24.3 0.0 collective-permute-done.other
  24.4 0.3 shard_map.97
  24.7 11.8 %all_to_all.5.arrived = bf16[32,24,128]{2,1,0:T(8,128)(2,1)S(1)} all-to-all(bf16[32,24,128]{2,1,0:T(8,128)(2,1)S(1)} %shard_map.97), channel_id=1, replica_groups={{26,27,24,25,30,31,28,29,18,19,16,17,22,23,20,21,10,11,8,9,14,15,12,13,..., dimensions={0} | all-to-all | bytes 393216 | tf_op jit(solution)/shard_map/all_to_all | solution.py:288
  36.5 0.8 %shard_map.98 = (bf16[1,4,4096]{2,1,0:T(4,128)(2,1)}, bf16[1,4,4096]{2,1,0:T(4,128)(2,1)}, bf16[1,4,4096]{2,1,0:T(4,128)(2,1)}, bf16[8,4096]{1,0:T(8,128)(2,1)}, f32[1,4]{1,0:T(1,128)}, /*index=5*/f32[8,8]{1,0:T(8,128)}) custom-call(bf16[32,24,128]{2,1,0:T(8,128)(2,1)S(1)} %all_to_all.5.arrived), custom_call_target="tpu_custom_call" | custom-call | flops 1048576 | tf_op jit(solution)/shard_map/pallas_call | solution.py:34
  (6 shorter events, 0.1 us)
Async XLA Ops:
  1.8 6.6 %collective-permute-start.1 = (f32[392,128]{1,0:T(8,128)S(1)}, f32[392,128]{1,0:T(8,128)S(1)}, u32[]{:S(2)}, u32[]{:S(2)}) collective-permute-start(f32[392,128]{1,0:T(8,128)S(1)} %get-tuple-element.30.sent), channel_id=1, source_target_pairs={{0,32},{32,0},{1,33},{33,1},{2,34},{34,2},{3,35},{35,3},{4,36},{36... | collective-permute-start | bytes 602120 | tf_op jit(solution)/shard_map/ppermute | solution.py:251
  6.6 6.4 %collective-permute-start.3 = (f32[768,128]{1,0:T(8,128)S(1)}, f32[768,128]{1,0:T(8,128)S(1)}, u32[]{:S(2)}, u32[]{:S(2)}) collective-permute-start(f32[768,128]{1,0:T(8,128)S(1)} %get-tuple-element.33), channel_id=1, source_target_pairs={{0,32},{32,0},{1,33},{33,1},{2,34},{34,2},{3,35},{35,3},{4,36},{36... | collective-permute-start | bytes 1179656 | tf_op jit(solution)/shard_map/ppermute | solution.py:259
  7.9 16.5 %collective-permute-start = (f32[384,128]{1,0:T(8,128)S(1)}, f32[384,128]{1,0:T(8,128)S(1)}, u32[]{:S(2)}, u32[]{:S(2)}) collective-permute-start(f32[384,128]{1,0:T(8,128)S(1)} %get-tuple-element.28), channel_id=1, source_target_pairs={{0,32},{32,0},{1,33},{33,1},{2,34},{34,2},{3,35},{35,3},{4,36},{36... | collective-permute-start | bytes 589832 | tf_op jit(solution)/shard_map/ppermute | solution.py:267
  8.6 8.7 %collective-permute-start.2 = (f16[400,128]{1,0:T(8,128)(2,1)S(1)}, f16[400,128]{1,0:T(8,128)(2,1)S(1)}, u32[]{:S(2)}, u32[]{:S(2)}) collective-permute-start(f16[400,128]{1,0:T(8,128)(2,1)S(1)} %get-tuple-element.47), channel_id=1, source_target_pairs={{0,192},{64,128},{128,0},{192,64},{1,193},{65,129},{129,1},{193,65... | collective-permute-start | bytes 307208 | tf_op jit(solution)/shard_map/ppermute | solution.py:271
  13.1 11.2 %collective-permute-start.4 = (f16[400,128]{1,0:T(8,128)(2,1)S(1)}, f16[400,128]{1,0:T(8,128)(2,1)S(1)}, u32[]{:S(2)}, u32[]{:S(2)}) collective-permute-start(f16[400,128]{1,0:T(8,128)(2,1)S(1)} %convert_element_type.24), channel_id=1, source_target_pairs={{0,64},{64,0},{128,192},{192,128},{1,65},{65,1},{129,193},{193,129... | collective-permute-start | bytes 307208 | tf_op jit(solution)/shard_map/ppermute | solution.py:271
  14.4 9.9 %collective-permute-start.5 = (f16[400,128]{1,0:T(8,128)(2,1)S(1)}, f16[400,128]{1,0:T(8,128)(2,1)S(1)}, u32[]{:S(2)}, u32[]{:S(2)}) collective-permute-start(f16[400,128]{1,0:T(8,128)(2,1)S(1)} %convert_element_type.26), channel_id=1, source_target_pairs={{0,128},{64,192},{128,64},{192,0},{1,129},{65,193},{129,65},{193,1... | collective-permute-start | bytes 307208 | tf_op jit(solution)/shard_map/ppermute | solution.py:271

commit v6 on v5

--- a/solution.py
+++ b/solution.py
@@ -164,6 +164,14 @@
     small[...] = total
 
 
+def decode_first(message, values):
+    rows = message.shape[0]
+    hidden = (rows - 16) // 3
+    for t in range(3):
+        values[t * hidden : (t + 1) * hidden, :] = read(message, t)
+    values[rows - 16 :, :] = message[rows - 16 :, :]
+
+
 def combine(peers, lines, kept, other, plus, far, minus, message, counted, out, held):
     line, core = lax.axis_index("zh"), lax.axis_index("c")
     rows, width = kept.shape
@@ -173,7 +181,7 @@
     for t in range(3):
         part = pl.ds(t * hidden, hidden)
         soup = kept[part, :] + other[part, :]
-        soup = (soup + read(far, t)) + (read(plus, t) + read(minus, t))
+        soup = (soup + read(far, t)) + (plus[part, :] + read(minus, t))
         held[part, :] = (soup * factor).astype(jnp.bfloat16).astype(F32)
     gates = [read(ref, 3) for ref in (message, far, plus, minus)]
     serve_gate = (((gates[0] + gates[1]) + (gates[2] + gates[3])) * factor).astype(jnp.bfloat16)
@@ -279,12 +287,13 @@
     came[STEPS[1]] = along(plus, STEPS[1])
     came[STEPS[2]] = along(minus, STEPS[2])
     counted = call(count, array((4, width)), 1 << 20)(far_parts, near_parts, own_parts, gate_parts)
+    early = call(decode_first, array((rows + 16, width)), 1 << 20)(came[1])
     message = call(
         functools.partial(combine, peers, lines),
         array((peers, experts + 3 * each + 4, width), jnp.bfloat16),
         1 << 22,
         (pltpu.VMEM((rows, width), F32),),
-    )(own_kept, own_came, came[1], came[2], came[3], far.astype(jnp.float16).astype(F32), counted)
+    )(own_kept, own_came, early, came[2], came[3], far.astype(jnp.float16).astype(F32), counted)
     arrived = lax.all_to_all(
         message, SA, 0, 0, axis_index_groups=[[peer ^ FIRST for peer in range(peers)]], tiled=True
     )

time: 37.5 us -> 37.5 us (level)
    pallas_call x8 -> x9, Pallas kernels: 5.27 us -> 5.29 us  [run(): pl.pallas_call(kernel, out_shape=out_shape, in_specs=specs, out_specs=jax...]
where the time goes in v6:
time: 37.5 us; the launch traced here: 37.2 us
  blocking collectives  11.8 us (31%)
  starting transfers between devices  10.9 us (29%)
  waiting for transfers between devices  8.45 us (23%)
  Pallas kernels  5.29 us (14%)
  between operations  0.74 us (2%)
    all_to_all x1, blocking collectives, steps(): lax.all_to_all(message, SA, 0, 0, axis_index_groups=[[peer ^ FIRST for pe...  11.8 us
    ppermute x3, waiting for transfers between devices, along(): return lax.ppermute(message.astype(jnp.float16), 'zh', pairs).astype(F32)  8.45 us
    ppermute x3, starting transfers between devices, along(): return lax.ppermute(message.astype(jnp.float16), 'zh', pairs).astype(F32)  6.9 us
    pallas_call x9, Pallas kernels, run(): pl.pallas_call(kernel, out_shape=out_shape, in_specs=specs, out_specs=jax...  5.29 us
    ppermute x1, starting transfers between devices, steps(): far_came = lax.ppermute(far_sent, 'c', swap)  3.29 us
  transfers between devices with their start and end apart: 6, of which 2 were waited for; matrix products, arithmetic and copies ran while one was open for 0% of the time, Pallas kernels for 8%

profile of v6, /device:TPU:1, one launch (start us, length us, event | category | flops | bytes accessed | tf_op | source)
XLA Modules:
  0.0 37.2 jit_solution(9403857480832550441)
XLA Ops:
  0.6 1.2 %shard_map.91 = (f32[392,128]{1,0:T(8,128)S(1)}, f32[384,128]{1,0:T(8,128)S(1)}, f32[1,2,3,2,8,128]{5,4,3,2,1,0:T(8,128)S(1)}, f32[2,8,128]{2,1,0:T(8,128)S(1)}) custom-call(f32[2,8,128,128]{3,2,1,0:T(8,128)} %refs_0_.5, f32[2,8,128,128]{3,2,1,0:T(8,128)} %refs_1_.5, f32[2,8,128,128]{3,2,1,0:T(8,128)} %refs_2_.5, f32[2,8,128]{2,1,0:T(8,128)} %refs_3_.1), custom_call_target="tpu_custom_call" | custom-call | flops 4194304 | tf_op jit(solution)/shard_map/pallas_call | solution.py:34
  1.8 3.3 %collective-permute-start.1 = (f32[392,128]{1,0:T(8,128)S(1)}, f32[392,128]{1,0:T(8,128)S(1)}, u32[]{:S(2)}, u32[]{:S(2)}) collective-permute-start(f32[392,128]{1,0:T(8,128)S(1)} %get-tuple-element.30.sent), channel_id=1, source_target_pairs={{0,32},{32,0},{1,33},{33,1},{2,34},{34,2},{3,35},{35,3},{4,36},{36... | collective-permute-start | bytes 602120 | tf_op jit(solution)/shard_map/ppermute | solution.py:259
  5.1 1.4 %shard_map.95 = (f32[768,128]{1,0:T(8,128)S(1)}, f32[768,128]{1,0:T(8,128)S(1)}, f32[2,2,3,2,8,128]{5,4,3,2,1,0:T(8,128)S(1)}) custom-call(f32[2,8,128,128]{3,2,1,0:T(8,128)} %refs_0_.5, f32[2,8,128,128]{3,2,1,0:T(8,128)} %refs_1_.5, f32[2,8,128,128]{3,2,1,0:T(8,128)} %refs_2_.5, f32[2,8,128]{2,1,0:T(8,128)S(1)} %get-tuple-element.26.refs_3_.gate_parts), custom_call_target="tpu_custom_call" | custom-call | flops 8388608 | tf_op jit(solution)/shard_map/pallas_call | solution.py:34
  6.6 0.1 collective-permute-start.3
  6.7 1.2 %shard_map.92 = (f32[384,128]{1,0:T(8,128)S(1)}, f32[384,128]{1,0:T(8,128)S(1)}, f32[1,2,3,2,8,128]{5,4,3,2,1,0:T(8,128)S(1)}) custom-call(f32[2,8,128,128]{3,2,1,0:T(8,128)} %refs_0_.5, f32[2,8,128,128]{3,2,1,0:T(8,128)} %refs_1_.5, f32[2,8,128,128]{3,2,1,0:T(8,128)} %refs_2_.5, f32[2,8,128]{2,1,0:T(8,128)S(1)} %get-tuple-element.26.refs_3_.gate_parts), custom_call_target="tpu_custom_call" | custom-call | flops 4194304 | tf_op jit(solution)/shard_map/pallas_call | solution.py:34
  7.9 0.6 %collective-permute-start = (f32[384,128]{1,0:T(8,128)S(1)}, f32[384,128]{1,0:T(8,128)S(1)}, u32[]{:S(2)}, u32[]{:S(2)}) collective-permute-start(f32[384,128]{1,0:T(8,128)S(1)} %get-tuple-element.28), channel_id=1, source_target_pairs={{0,32},{32,0},{1,33},{33,1},{2,34},{34,2},{3,35},{35,3},{4,36},{36... | collective-permute-start | bytes 589832 | tf_op jit(solution)/shard_map/ppermute | solution.py:275
  8.4 0.0 collective-permute-done.1.came
  8.4 0.1 shard_map.93
  8.6 4.4 %collective-permute-start.2 = (f16[400,128]{1,0:T(8,128)(2,1)S(1)}, f16[400,128]{1,0:T(8,128)(2,1)S(1)}, u32[]{:S(2)}, u32[]{:S(2)}) collective-permute-start(f16[400,128]{1,0:T(8,128)(2,1)S(1)} %get-tuple-element.47), channel_id=1, source_target_pairs={{0,192},{64,128},{128,0},{192,64},{1,193},{65,129},{129,1},{193,65... | collective-permute-start | bytes 307208 | tf_op jit(solution)/shard_map/ppermute | solution.py:279
  12.9 0.0 collective-permute-done.3.came
  12.9 0.1 shard_map.96
  13.1 1.3 %collective-permute-start.4 = (f16[400,128]{1,0:T(8,128)(2,1)S(1)}, f16[400,128]{1,0:T(8,128)(2,1)S(1)}, u32[]{:S(2)}, u32[]{:S(2)}) collective-permute-start(f16[400,128]{1,0:T(8,128)(2,1)S(1)} %convert_element_type.24), channel_id=1, source_target_pairs={{0,64},{64,0},{128,192},{192,128},{1,65},{65,1},{129,193},{193,129... | collective-permute-start | bytes 307208 | tf_op jit(solution)/shard_map/ppermute | solution.py:279
  14.4 1.2 %collective-permute-start.5 = (f16[400,128]{1,0:T(8,128)(2,1)S(1)}, f16[400,128]{1,0:T(8,128)(2,1)S(1)}, u32[]{:S(2)}, u32[]{:S(2)}) collective-permute-start(f16[400,128]{1,0:T(8,128)(2,1)S(1)} %convert_element_type.26), channel_id=1, source_target_pairs={{0,128},{64,192},{128,64},{192,0},{1,129},{65,193},{129,65},{193,1... | collective-permute-start | bytes 307208 | tf_op jit(solution)/shard_map/ppermute | solution.py:279
  15.6 0.1 shard_map.97.counted
  15.8 1.4 %collective-permute-done.2 = f16[400,128]{1,0:T(8,128)(2,1)S(1)} collective-permute-done((f16[400,128]{1,0:T(8,128)(2,1)S(1)}, f16[400,128]{1,0:T(8,128)(2,1)S(1)}, u32[]{:S(2)}, u32[]{:S(2)}) %collective-permute-start.2) | collective-permute-done | bytes 102432 | tf_op jit(solution)/shard_map/ppermute | solution.py:279
  17.3 7.0 %collective-permute-done.4 = f16[400,128]{1,0:T(8,128)(2,1)S(1)} collective-permute-done((f16[400,128]{1,0:T(8,128)(2,1)S(1)}, f16[400,128]{1,0:T(8,128)(2,1)S(1)}, u32[]{:S(2)}, u32[]{:S(2)}) %collective-permute-start.4) | collective-permute-done | bytes 102432 | tf_op jit(solution)/shard_map/ppermute | solution.py:279
  24.3 0.0 collective-permute-done.5
  24.3 0.0 collective-permute-done.other
  24.4 0.3 shard_map.98
  24.7 11.8 %all_to_all.5.arrived = bf16[32,24,128]{2,1,0:T(8,128)(2,1)S(1)} all-to-all(bf16[32,24,128]{2,1,0:T(8,128)(2,1)S(1)} %shard_map.98), channel_id=1, replica_groups={{26,27,24,25,30,31,28,29,18,19,16,17,22,23,20,21,10,11,8,9,14,15,12,13,..., dimensions={0} | all-to-all | bytes 393216 | tf_op jit(solution)/shard_map/all_to_all | solution.py:297
  36.4 0.8 %shard_map.99 = (bf16[1,4,4096]{2,1,0:T(4,128)(2,1)}, bf16[1,4,4096]{2,1,0:T(4,128)(2,1)}, bf16[1,4,4096]{2,1,0:T(4,128)(2,1)}, bf16[8,4096]{1,0:T(8,128)(2,1)}, f32[1,4]{1,0:T(1,128)}, /*index=5*/f32[8,8]{1,0:T(8,128)}) custom-call(bf16[32,24,128]{2,1,0:T(8,128)(2,1)S(1)} %all_to_all.5.arrived), custom_call_target="tpu_custom_call" | custom-call | flops 1048576 | tf_op jit(solution)/shard_map/pallas_call | solution.py:34
  (7 shorter events, 0.2 us)
Async XLA Ops:
  1.8 6.6 %collective-permute-start.1 = (f32[392,128]{1,0:T(8,128)S(1)}, f32[392,128]{1,0:T(8,128)S(1)}, u32[]{:S(2)}, u32[]{:S(2)}) collective-permute-start(f32[392,128]{1,0:T(8,128)S(1)} %get-tuple-element.30.sent), channel_id=1, source_target_pairs={{0,32},{32,0},{1,33},{33,1},{2,34},{34,2},{3,35},{35,3},{4,36},{36... | collective-permute-start | bytes 602120 | tf_op jit(solution)/shard_map/ppermute | solution.py:259
  6.6 6.4 %collective-permute-start.3 = (f32[768,128]{1,0:T(8,128)S(1)}, f32[768,128]{1,0:T(8,128)S(1)}, u32[]{:S(2)}, u32[]{:S(2)}) collective-permute-start(f32[768,128]{1,0:T(8,128)S(1)} %get-tuple-element.33), channel_id=1, source_target_pairs={{0,32},{32,0},{1,33},{33,1},{2,34},{34,2},{3,35},{35,3},{4,36},{36... | collective-permute-start | bytes 1179656 | tf_op jit(solution)/shard_map/ppermute | solution.py:267
  7.9 16.5 %collective-permute-start = (f32[384,128]{1,0:T(8,128)S(1)}, f32[384,128]{1,0:T(8,128)S(1)}, u32[]{:S(2)}, u32[]{:S(2)}) collective-permute-start(f32[384,128]{1,0:T(8,128)S(1)} %get-tuple-element.28), channel_id=1, source_target_pairs={{0,32},{32,0},{1,33},{33,1},{2,34},{34,2},{3,35},{35,3},{4,36},{36... | collective-permute-start | bytes 589832 | tf_op jit(solution)/shard_map/ppermute | solution.py:275
  8.6 8.7 %collective-permute-start.2 = (f16[400,128]{1,0:T(8,128)(2,1)S(1)}, f16[400,128]{1,0:T(8,128)(2,1)S(1)}, u32[]{:S(2)}, u32[]{:S(2)}) collective-permute-start(f16[400,128]{1,0:T(8,128)(2,1)S(1)} %get-tuple-element.47), channel_id=1, source_target_pairs={{0,192},{64,128},{128,0},{192,64},{1,193},{65,129},{129,1},{193,65... | collective-permute-start | bytes 307208 | tf_op jit(solution)/shard_map/ppermute | solution.py:279
  13.1 11.2 %collective-permute-start.4 = (f16[400,128]{1,0:T(8,128)(2,1)S(1)}, f16[400,128]{1,0:T(8,128)(2,1)S(1)}, u32[]{:S(2)}, u32[]{:S(2)}) collective-permute-start(f16[400,128]{1,0:T(8,128)(2,1)S(1)} %convert_element_type.24), channel_id=1, source_target_pairs={{0,64},{64,0},{128,192},{192,128},{1,65},{65,1},{129,193},{193,129... | collective-permute-start | bytes 307208 | tf_op jit(solution)/shard_map/ppermute | solution.py:279
  14.4 9.9 %collective-permute-start.5 = (f16[400,128]{1,0:T(8,128)(2,1)S(1)}, f16[400,128]{1,0:T(8,128)(2,1)S(1)}, u32[]{:S(2)}, u32[]{:S(2)}) collective-permute-start(f16[400,128]{1,0:T(8,128)(2,1)S(1)} %convert_element_type.26), channel_id=1, source_target_pairs={{0,128},{64,192},{128,64},{192,0},{1,129},{65,193},{129,65},{193,1... | collective-permute-start | bytes 307208 | tf_op jit(solution)/shard_map/ppermute | solution.py:279
